TPU v7x, 128 devices: a whole 4x4x4 slice. The times are simulated.
128 devices in a mesh: data: 1, col: 64 (over z, y, x), dap: 2 (over core).
Axes of the slice: x: 4, y: 4, z: 4, core: 2. Of those that a mesh axis runs over, the one named last changes fastest.
Arguments:
- msa_act: bfloat16 [1024, 768, 256], P(('data', 'dap'), 'col')
- msa_mask: int32 [1024, 768], P(('data', 'dap'), 'col')
- pair_act: float32 [768, 768, 128], P(('data', 'dap'), 'col')
- ln_gamma: bfloat16 [256], replicated
- ln_beta: bfloat16 [256], replicated
- w_a: bfloat16 [256, 32], replicated
- b_a: bfloat16 [32], replicated
- w_b: bfloat16 [256, 32], replicated
- b_b: bfloat16 [32], replicated
- w_out: bfloat16 [1024, 128], replicated
- b_out: bfloat16 [128], replicated
Outputs:
- output: float32 [768, 768, 128], P(('data', 'dap'), 'col')
All inputs are finite; a program needn't handle non-finite values.
Results may differ from a plain program's by a relative error of at most 0.00129929.
Values are sent between devices in bfloat16 or wider.
A program may use at most 1 GiB of HBM per device.

v0:
```python
import jax
import jax.numpy as jnp
from jax import lax
from jax.sharding import PartitionSpec as P


def layer_norm(value_a7, ln_gamma, ln_beta):
    values_f = value_a7.astype(jnp.float32)
    mean_val = jnp.mean(values_f, axis=-1, keepdims=True)
    centred = values_f - mean_val
    variance = jnp.mean(centred * centred, axis=-1, keepdims=True)
    normed = centred * lax.rsqrt(variance + 1e-5)
    return (normed * ln_gamma.astype(jnp.float32) + ln_beta.astype(jnp.float32)).astype(jnp.bfloat16)


def project(normed, mask_col, weight, bias_vec):
    lin = jnp.einsum('snm,mc->snc', normed, weight, preferred_element_type=jnp.float32)
    return ((lin + bias_vec.astype(jnp.float32)) * mask_col).astype(jnp.bfloat16)


def solution(mesh):
    row_spec = P(('data', 'dap'), 'col', None)
    mask_spec = P(('data', 'dap'), 'col')
    in_specs = (row_spec, mask_spec, row_spec) + (P(),) * 8

    def local_fn(value_a7, value_a8, pair_act, ln_gamma, ln_beta, w_a, b_a, w_b, b_b, w_out, b_out):
        hidden = w_a.shape[1]
        pair_dim = w_out.shape[1]
        normed = layer_norm(value_a7, ln_gamma, ln_beta)
        mask_bf = value_a8.astype(jnp.bfloat16)
        proj_a = project(normed, mask_bf[:, :, None], w_a, b_a)
        proj_b = project(normed, mask_bf[:, :, None], w_b, b_b)
        full_a = lax.all_gather(proj_a, 'col', axis=1, tiled=True)
        full_mask = lax.all_gather(mask_bf, 'col', axis=1, tiled=True)
        w_cube = w_out.reshape(hidden, hidden, pair_dim)
        proj_bw = jnp.einsum('sjd,cdz->scjz', proj_b, w_cube, preferred_element_type=jnp.float32).astype(jnp.bfloat16)
        part_sum = jnp.einsum('sic,scjz->ijz', full_a, proj_bw, preferred_element_type=jnp.float32)
        part_norm = jnp.einsum('si,sj->ij', full_mask, mask_bf, preferred_element_type=jnp.float32)
        row_sum = lax.psum_scatter(part_sum, 'dap', scatter_dimension=0, tiled=True)
        row_norm = lax.psum_scatter(part_norm, 'dap', scatter_dimension=0, tiled=True)
        return pair_act + (row_sum + b_out.astype(jnp.float32)) / (1e-3 + row_norm)[:, :, None]

    return jax.shard_map(local_fn, mesh=mesh, in_specs=in_specs, out_specs=row_spec, check_vma=False)
```

profile of v0, /device:TPU:1, one launch (start us, length us, event | category | flops | bytes accessed | tf_op | source)
XLA Modules:
  0.0 305.8 jit_solution(11778848425506985158)
XLA Ops:
  7.4 0.0 copy-start
  7.4 0.0 all-gather.3.cloned.1.call-start
  7.4 0.0 copy-start.6
  7.4 0.0 copy-start.7
  7.4 0.0 copy-start.8
  7.4 0.0 copy-start.5
  7.4 2.9 convert_reduce_fusion
  10.4 3.3 %fusion.9 = f32[512,12]{0,1:T(8,128)S(1)} fusion(bf16[512,12,256]{2,0,1:T(8,128)(2,1)} %param.11, f32[512,12]{0,1:T(8,128)S(1)} %broadcast_multiply_fusion), kind=kLoop, calls=%fused_computation.10 | loop fusion | flops 6285312 | bytes 3194880 | tf_op jit(solution)/shard_map/reduce_sum | solution.py:11
  13.7 0.0 copy-done.4
  13.7 0.0 copy-done.6
  13.7 0.0 copy-done.7
  13.8 0.5 copy-done.10
  14.3 0.0 copy-done.2
  14.3 3.2 %fusion.37 = bf16[512,12,32]{0,2,1:T(8,128)(2,1)} fusion(bf16[512,12,256]{2,0,1:T(8,128)(2,1)S(1)} %copy-done.2, f32[256]{0:T(256)S(1)} %convert_element_type.43, f32[256]{0:T(256)S(1)} %convert_element_type.42, f32[512,12]{0,1:T(8,128)S(1)} %add_rsqrt_fusion, f32[512,12]{0,1:T(8,128)S(1)} %broadcast_multiply_fusion, f32[512,12]{0,1:T(8,128)S(1)} %get-tuple-element.6, ...), kind=kOutput, calls=%fused_computation.23 | convolution fusion | flops 110690304 | bytes 3631232 | tf_op jit(solution)/shard_map/snm,mc->snc/dot_general | solution.py:17
  17.5 0.0 all-gather.3.cloned.1.call-update
  17.5 0.0 reduce-scatter.5.cloned.1.call-start
  17.5 164.8 %all-gather = bf16[64,12,512]{2,1,0:T(8,128)(2,1)} all-gather(bf16[1,12,512]{2,1,0:T(8,128)(2,1)S(1)} %get-tuple-element.5), channel_id=1, replica_groups=mesh['data'=1,'col'=64,'dap'=2] {'col'}, dimensions={0}, use_global_device_ids=true | all-gather | bytes 798720 | tf_op jit(solution)/shard_map/all_gather | solution.py:34
  182.4 2.1 reshape.25
  184.4 2.1 fusion.45
  186.5 0.0 reduce-scatter.5.cloned.1.call-update
  186.5 0.0 reduce-scatter.3.cloned.1.call-start
  186.6 0.7 convert_element_type.49
  187.2 3.2 %fusion.40 = bf16[512,12,32,1]{0,2,3,1:T(8,128)(2,1)S(1)} fusion(bf16[512,12,256]{2,0,1:T(8,128)(2,1)S(1)} %copy-done.2, f32[256]{0:T(256)} %copy-done.11, f32[256]{0:T(256)} %copy-done.10, f32[512,12]{0,1:T(8,128)S(1)} %add_rsqrt_fusion, f32[512,12]{0,1:T(8,128)S(1)} %broadcast_multiply_fusion, f32[32]{0:T(128)S(1)} %convert_element_type.49, ...), kind=kOutput, calls=%fused_computation.24 | convolution fusion | flops 110690304 | bytes 3631232 | tf_op jit(solution)/shard_map/snm,mc->snc/dot_general | solution.py:17
  190.5 19.7 %fusion.59 = bf16[512,32,12,128]{3,0,1,2:T(8,128)(2,1)} fusion(bf16[512,12,32,1]{0,2,3,1:T(8,128)(2,1)S(1)} %fusion.40, bf16[32,32,128,1]{2,1,0,3:T(8,128)(2,1)S(1)} %bitcast.45), kind=kOutput, calls=%fused_computation.1.clone.clone.clone.1 | convolution fusion | flops 1635778560 | bytes 50987008 | tf_op jit(solution)/shard_map/sjd,cdz->scjz/dot_general | solution.py:36
  210.2 51.8 %fusion.13 = f32[768,12,128]{2,0,1:T(8,128)} fusion(bf16[512,768,32]{0,2,1:T(8,128)(2,1)} %all-gather.3.cloned.1.call-done, bf16[512,32,12,128]{3,0,1,2:T(8,128)(2,1)} %fusion.59), kind=kOutput, calls=%fused_computation.15 | convolution fusion | flops 38654705664 | bytes 80216064 | tf_op jit(solution)/shard_map/sic,scjz->ijz/dot_general | solution.py:37
  262.0 0.0 reduce-scatter.3.cloned.1.call-update
  262.0 0.0 copy-done.9
  262.0 0.0 reduce-scatter.5.cloned.1.call-done
  262.1 0.9 broadcast_add_fusion
  263.0 32.4 %reduce-scatter.3.cloned.1.call-done = f32[384,12,128]{2,0,1:T(8,128)} async-done(((f32[768,12,128]{2,0,1:T(8,128)}), f32[384,12,128]{2,0,1:T(8,128)}) %reduce-scatter.3.cloned.1.call-update) | async-done | bytes 2359312 | tf_op jit(solution)/shard_map/reduce_scatter | solution.py:39
  295.3 0.0 copy-done.3
  295.3 3.1 %divide_add_fusion = f32[384,12,128]{2,0,1:T(8,128)} fusion(f32[384,12,128]{2,0,1:T(8,128)S(1)} %copy-done.3, f32[384,12,128]{2,0,1:T(8,128)} %reduce-scatter.3.cloned.1.call-done, f32[384,12]{0,1:T(8,128)S(1)} %broadcast_add_fusion, f32[128]{0:T(128)S(1)} %convert_element_type.53), kind=kLoop, calls=%fused_computation.14 | loop fusion | flops 1769472 | bytes 7096832 | tf_op jit(solution)/shard_map/add | solution.py:41
  (20 shorter events, 0.1 us)
Async XLA Ops:
  7.4 183.1 %copy-start = (bf16[1024,128]{1,0:T(8,128)(2,1)S(1)}, bf16[1024,128]{1,0:T(8,128)(2,1)}, u32[]{:S(2)}) copy-start(bf16[1024,128]{1,0:T(8,128)(2,1)} %param.20) | copy-start | bytes 786436
  7.4 6.9 %copy-start.2 = (bf16[512,12,256]{2,0,1:T(8,128)(2,1)S(1)}, bf16[512,12,256]{2,0,1:T(8,128)(2,1)}, u32[]{:S(2)}) copy-start(bf16[512,12,256]{2,0,1:T(8,128)(2,1)} %param.11) | copy-start | bytes 9437188
  7.4 6.3 %copy-start.4 = (s32[512,12]{0,1:T(8,128)S(1)}, s32[512,12]{0,1:T(8,128)}, u32[]{:S(2)}) copy-start(s32[512,12]{0,1:T(8,128)} %param.12) | copy-start | bytes 73732
  7.4 202.8 %all-gather.3.cloned.1.call-start = ((), (), s32[]{:S(2)}) async-start(), calls=%async_computation.2 | async-start | bytes 25559040 | tf_op jit(solution)/shard_map/all_gather | solution.py:33
  7.4 6.3 %copy-start.6 = (bf16[256]{0:T(256)(128)(2,1)S(1)}, bf16[256]{0:T(256)(128)(2,1)}, u32[]{:S(2)}) copy-start(bf16[256]{0:T(256)(128)(2,1)} %param.14) | copy-start | bytes 1540
  7.4 6.3 %copy-start.7 = (bf16[256]{0:T(256)(128)(2,1)S(1)}, bf16[256]{0:T(256)(128)(2,1)}, u32[]{:S(2)}) copy-start(bf16[256]{0:T(256)(128)(2,1)} %param.15) | copy-start | bytes 1540
  7.4 6.3 %copy-start.8 = (bf16[32]{0:T(256)(128)(2,1)S(1)}, bf16[32]{0:T(256)(128)(2,1)}, u32[]{:S(2)}) copy-start(bf16[32]{0:T(256)(128)(2,1)} %param.17) | copy-start | bytes 196
  7.4 6.9 %copy-start.5 = (bf16[256,32]{0,1:T(8,128)(2,1)S(1)}, bf16[256,32]{0,1:T(8,128)(2,1)}, u32[]{:S(2)}) copy-start(bf16[256,32]{0,1:T(8,128)(2,1)} %param.16) | copy-start | bytes 49156
  13.7 0.6 copy-start.10
  13.7 0.5 copy-start.11
  17.5 244.6 %reduce-scatter.5.cloned.1.call-start = ((), (), s32[]{:S(2)}) async-start(), calls=%async_computation.4 | async-start | bytes 73728 | tf_op jit(solution)/shard_map/reduce_scatter | solution.py:40
  186.5 108.8 %reduce-scatter.3.cloned.1.call-start = ((), (), s32[]{:S(2)}) async-start(), calls=%async_computation.3 | async-start | bytes 7077888 | tf_op jit(solution)/shard_map/reduce_scatter | solution.py:39
  210.2 51.8 %copy-start.9 = (bf16[128]{0:T(256)(128)(2,1)S(1)}, bf16[128]{0:T(256)(128)(2,1)}, u32[]{:S(2)}) copy-start(bf16[128]{0:T(256)(128)(2,1)} %param.21) | copy-start | bytes 772
  210.2 88.2 %copy-start.1 = (bf16[1024,128]{1,0:T(8,128)(2,1)S(1)}, bf16[1024,128]{1,0:T(8,128)(2,1)}, u32[]{:S(2)}) copy-start(bf16[1024,128]{1,0:T(8,128)(2,1)} %param.20) | copy-start | bytes 786436
  262.0 33.3 %copy-start.3 = (f32[384,12,128]{2,0,1:T(8,128)S(1)}, f32[384,12,128]{2,0,1:T(8,128)}, u32[]{:S(2)}) copy-start(f32[384,12,128]{2,0,1:T(8,128)} %param.13) | copy-start | bytes 7077892
Sparse Core Ops, SparseCore 0:
  17.6 140.2 all-gather.2
Sparse Core Ops, SparseCore 1:
  186.6 28.8 reduce-scatter.4
  262.1 33.2 reduce-scatter.2
where the time goes:
time: 306 us
  blocking collectives  165 us (54%)
  matrix products  80 us (26%)
  waiting for transfers between devices  32.4 us (11%)
  between operations  15 us (5%)
  other arithmetic  10.9 us (4%)
    all_gather x1, blocking collectives, local_fn(): full_mask = lax.all_gather(mask_bf, 'col', axis=1, tiled=True)  165 us
    dot_general x1, matrix products, local_fn(): jnp.einsum('sic,scjz->ijz', full_a, proj_bw, preferred_element_type=jnp.f...  51.8 us
    reduce_scatter x1, waiting for transfers between devices, local_fn(): row_sum = lax.psum_scatter(part_sum, 'dap', scatter_dimension=0, tiled=True)  32.4 us
    dot_general x1, matrix products, local_fn(): jnp.einsum('sjd,cdz->scjz', proj_b, w_cube, preferred_element_type=jnp.fl...  19.7 us
    dot_general x2, matrix products, project(): jnp.einsum('snm,mc->snc', normed, weight, preferred_element_type=jnp.floa...  6.39 us
  transfers between devices with their start and end apart: 3, of which 1 were waited for; matrix products, arithmetic and copies ran while one was open for 26% of the time, Pallas kernels for 0%

commit v1 on v0

v1 whole, which is shorter than its diff:
```python
import jax
import jax.numpy as jnp
from jax import lax
from jax.experimental import pallas as pl
from jax.experimental.pallas import tpu as pltpu
from jax.sharding import PartitionSpec as P

F32 = jnp.float32
BF16 = jnp.bfloat16
MESH = pl.DeviceIdType.MESH
NT = (((1,), (1,)), ((), ()))

SEQ, RES, CH, HID, PAIR = 512, 12, 256, 32, 128
PIECE = 128
NP = SEQ // PIECE
AROWS = RES * HID
PROWS = AROWS + 16
UNIT = 2 * RES


def iota(shape, axis):
    return lax.broadcasted_iota(jnp.int32, shape, axis)


def dot(a, b, dims=None):
    if dims is None:
        return jnp.dot(a, b, preferred_element_type=F32)
    return lax.dot_general(a, b, dims, preferred_element_type=F32)


def kernel(m_hbm, mask_ref, z_hbm, gamma_ref, beta_ref, wa_ref, ba_ref, wb_ref, bb_ref, wo_ref, bo_ref,
           out_hbm,
           m_v, mask_v, wabig, b32, a_buf, b_buf, bt, lhs2, rt, w32, wo_p, r_send, r_recv, n_send, n_recv,
           mask_all, inv_v, z_v, out_v,
           m_sem, z_sem, o_sem, a_ss, a_rs, b_ss, b_rs, r_ss, r_rs, n_ss, n_rs):
    col = lax.axis_index("col")
    dap = lax.axis_index("dap")
    zz, yy, xx = col // 16, (col // 4) % 4, col % 4
    home = zz // 2
    other = 1 - dap

    def at(dz=0, dy=0, dx=0):
        return ((zz + dz) % 4) * 16 + ((yy + dy) % 4) * 4 + (xx + dx) % 4

    def dev(c, d):
        return {"col": c, "dap": d}

    for p in range(NP):
        pltpu.make_async_copy(m_hbm.at[:, pl.ds(PIECE * p, PIECE), :], m_v.at[p], m_sem.at[p]).start()
    barrier = pltpu.get_barrier_semaphore()
    greet = [dev(at(dy=1), dap), dev(at(dy=3), dap), dev(at(dx=1), dap), dev(at(dx=3), dap), dev(col, other)]
    for r in (1, 2, 3):
        for d in (0, 1):
            greet.append(dev(at(dz=r), d))
    for who in greet:
        pl.semaphore_signal(barrier, inc=1, device_id=who, device_id_type=MESH)

    mask_v[...] = jnp.zeros_like(mask_v)
    mask_v[0:RES, :] = mask_ref[...].astype(F32)
    wa = wa_ref[...]
    for k in range(4):
        rows = [wa if kk == k else jnp.zeros_like(wa) for kk in range(4)]
        wabig[:, CH * k:CH * (k + 1)] = jnp.concatenate(rows, axis=0)
    gamma = gamma_ref[...].astype(F32)
    beta = beta_ref[...].astype(F32)
    tile4 = jnp.where(iota((HID, 128), 1) % HID == iota((HID, 128), 0), 1.0, 0.0).astype(BF16)
    ba_row = dot(jnp.broadcast_to(ba_ref[...], (16, HID)), tile4)[0:1, :]
    eye = iota((HID, HID), 0) == iota((HID, HID), 1)
    bb_diag = jnp.where(eye, jnp.broadcast_to(bb_ref[...], (HID, HID)).astype(F32), 0.0).astype(BF16)
    bb_col = dot(bb_diag, jnp.ones((HID, 128), BF16))

    def a_copy(slot, p, way):
        dy, dx = slot
        sy, sx = {"x+": (0, 1), "x-": (0, -1), "y+": (1, 0), "y-": (-1, 0)}[way]
        to = ((dy + sy) % 4) * 4 + (dx + sx) % 4
        w = {"x+": 0, "x-": 1, "y+": 2, "y-": 3}[way]
        here = dy * 4 + dx
        return pltpu.make_async_remote_copy(
            src_ref=a_buf.at[here, p], dst_ref=a_buf.at[to, p], send_sem=a_ss.at[here, p, w],
            recv_sem=a_rs.at[to, p], device_id=dev(at(dy=sy, dx=sx), dap), device_id_type=MESH)

    def b_copy(r, p, way):
        s = 1 if way == "z+" else -1
        to = (r + s) % 4
        return pltpu.make_async_remote_copy(
            src_ref=b_buf.at[r, p], dst_ref=b_buf.at[to, p], send_sem=b_ss.at[r, p, 0 if s == 1 else 1],
            recv_sem=b_rs.at[to, p], device_id=dev(at(dz=s), dap), device_id_type=MESH)

    a_sent, b_sent = [], []

    def send_a(slot, p, way):
        a_copy(slot, p, way).start()
        a_sent.append((slot, p, way))

    def send_b(r, p, way):
        b_copy(r, p, way).start()
        b_sent.append((r, p, way))

    def wait_a(slot, p):
        i = slot[0] * 4 + slot[1]
        pltpu.make_async_remote_copy(
            src_ref=a_buf.at[i, p], dst_ref=a_buf.at[i, p], send_sem=a_ss.at[i, p, 0], recv_sem=a_rs.at[i, p],
            device_id=dev(at(dx=1), dap), device_id_type=MESH).wait_recv()

    def wait_b(r, p):
        pltpu.make_async_remote_copy(
            src_ref=b_buf.at[r, p], dst_ref=b_buf.at[r, p], send_sem=b_ss.at[r, p, 0], recv_sem=b_rs.at[r, p],
            device_id=dev(at(dz=1), dap), device_id_type=MESH).wait_recv()

    def project(p, carry):
        pltpu.make_async_copy(m_hbm.at[:, pl.ds(0, PIECE), :], m_v.at[p], m_sem.at[p]).wait()
        lanes = pl.ds(pl.multiple_of(PIECE * p, PIECE), PIECE)
        mask_p = mask_v[:, lanes]
        mask_b = mask_p.astype(BF16)
        mask_t = mask_p.T.astype(BF16)
        for q in range(3):
            xs = []
            for k in range(4):
                n = 4 * q + k
                v = m_v[p, n].astype(F32)
                mean = jnp.sum(v, axis=1, keepdims=True) * (1.0 / CH)
                cen = v - mean
                var = jnp.sum(cen * cen, axis=1, keepdims=True) * (1.0 / CH)
                x = (cen * lax.rsqrt(var + 1e-5) * gamma + beta).astype(BF16)
                xs.append(x)
                lin_b = dot(wb_ref[...], x, NT)
                b32[pl.ds(n, HID, stride=RES), :] = (lin_b + bb_col) * mask_p[n:n + 1, :]
            lin_a = dot(jnp.concatenate(xs, axis=1), wabig[...], NT)
            spread = jnp.where(iota((16, 128), 1) // HID + 4 * q == iota((16, 128), 0), 1.0, 0.0).astype(BF16)
            a_buf[0, p, 128 * q:128 * (q + 1), :] = ((lin_a + ba_row) * dot(mask_t, spread)).astype(BF16)
        a_buf[0, p, AROWS:PROWS, :] = mask_b
        b_buf[0, p, 0:AROWS, :] = b32[...].astype(BF16)
        b_buf[0, p, AROWS:PROWS, :] = mask_b

        @pl.when(p == 0)
        def _():
            pl.semaphore_wait(barrier, len(greet))

        for way in ("z+", "z-"):
            b_copy(0, p, way).start()
        for way in ("x+", "x-", "y+", "y-"):
            a_copy((0, 0), p, way).start()
        return carry

    lax.fori_loop(0, NP, project, 0)
    for p in range(NP):
        b_sent += [(0, p, w) for w in ("z+", "z-")]
        a_sent += [((0, 0), p, w) for w in ("x+", "x-", "y+", "y-")]
    pltpu.make_async_copy(z_hbm, z_v, z_sem).start()

    early = []
    for p in (0, 1):
        wait_b(1, p)
        send_b(1, p, "z+")
        wait_b(3, p)
    for p in range(NP):
        fwd = p // 2 == 0
        if p >= 2:
            wait_b(3, p)
            send_b(3, p, "z-")
            wait_b(1, p)
        for d, on in ((1, "+"), (3, "-")):
            slot = (0, d) if p % 2 == 0 else (d, 0)
            wait_a(slot, p)
            early.append((slot, p))
            first, second = ("x", "y") if p % 2 == 0 else ("y", "x")
            if fwd == (d == 1):
                send_a(slot, p, first + on)
            send_a(slot, p, second + "+")
            send_a(slot, p, second + "-")

    w32[...] = wo_ref[...].astype(F32)

    def order(d, carry):
        wo_p[pl.ds(pl.multiple_of(HID * d, HID), HID), :] = w32[pl.ds(d, HID, stride=HID), :].astype(BF16)
        return carry

    lax.fori_loop(0, HID, order, 0)

    for p in range(NP):
        slot = (0, 2) if p % 2 == 0 else (2, 0)
        second = "y" if p % 2 == 0 else "x"
        wait_a(slot, p)
        early.append((slot, p))
        send_a(slot, p, second + "+")
        send_a(slot, p, second + "-")

    for p in range(NP):
        wait_b(2, p)
    n192 = 4 * 4 * RES
    ro, co = iota((n192, n192), 0), iota((n192, n192), 1)
    want = ((ro // RES) % 4) * 48 + (ro // 48) * RES + ro % RES
    perm = jnp.where(want == co, 1.0, 0.0).astype(BF16)

    def regroup(g, carry):
        rows = pl.ds(pl.multiple_of(48 * g, 16), 48)
        cat = jnp.concatenate(
            [jnp.concatenate([b_buf[r, p, rows, :] for p in range(NP)], axis=1) for r in range(4)], axis=0)
        bt[pl.ds(pl.multiple_of(n192 * g, 64), n192), :] = dot(perm, cat).astype(BF16)
        return carry

    lax.fori_loop(0, 8, regroup, 0)

    lane = iota((1, 128), 1)
    low = lane < 64
    odd = (lane // HID) % 2 == 1

    def transpose4(v):
        def swap(u, w):
            t = pltpu.roll(jnp.where(low, w, u), 64, 1)
            return jnp.where(low, u, t), jnp.where(low, t, w)

        def swap2(u, w):
            return (jnp.where(odd, pltpu.roll(w, 32, 1), u), jnp.where(odd, w, pltpu.roll(u, 96, 1)))

        e0, e2 = swap(v[0], v[2])
        e1, e3 = swap(v[1], v[3])
        w0, w1 = swap2(e0, e1)
        w2, w3 = swap2(e2, e3)
        return w0, w1, w2, w3

    def r_copy(t, r, unit):
        return pltpu.make_async_remote_copy(
            src_ref=r_send.at[t, r], dst_ref=r_recv.at[zz % 2, dap, unit], send_sem=r_ss.at[t, r],
            recv_sem=r_rs.at[zz % 2, dap, unit], device_id=dev(at(dz=-r), home), device_id_type=MESH)

    def n_copy(r):
        return pltpu.make_async_remote_copy(
            src_ref=n_send.at[r], dst_ref=n_recv.at[zz % 2, dap], send_sem=n_ss.at[r],
            recv_sem=n_rs.at[zz % 2, dap], device_id=dev(at(dz=-r), home), device_id_type=MESH)

    line = (0, 1, 3, 2)
    done = set(early)
    plan = {0: [], 2: [], 4: [], 6: []}
    for i, dy in enumerate(line):
        for dx in (0, 1, 3, 2):
            for p in range(NP):
                if (dy, dx) == (0, 0) or ((dy, dx), p) in done:
                    continue
                h, e = p % 2, p // 2
                on = None
                if h == 0 and dy == 1 and e == 0:
                    on = "y+"
                if h == 0 and dy == 3 and e == 1:
                    on = "y-"
                if h == 1 and dx == 1 and e == 0:
                    on = "x+"
                if h == 1 and dx == 3 and e == 1:
                    on = "x-"
                plan[2 * i].append(((dy, dx), p, on))

    def step(t, carry):
        for when, events in plan.items():
            @pl.when(t == when)
            def _(events=events):
                for slot, p, on in events:
                    wait_a(slot, p)
                    if on:
                        send_a(slot, p, on)

        lrel = t // 2
        dy = jnp.where(lrel == 2, 3, jnp.where(lrel == 3, 2, lrel))
        ys = (yy + 4 - dy) % 4
        pair = (xx // 2 + t % 2) % 2
        unit = ys * 2 + pair
        slots = [dy * 4 + (xx + 4 - (2 * pair + o)) % 4 for o in range(2)]

        def outer(g, c2):
            lhs = bt[pl.ds(pl.multiple_of(2 * n192 * g, 128), 2 * n192), :]
            for o in range(2):
                rhs = jnp.concatenate(
                    [jnp.concatenate([a_buf[slots[o], p, 128 * q:128 * (q + 1), :] for q in range(3)], axis=1)
                     for p in range(NP)], axis=0)
                prod = dot(lhs, rhs)
                for q in range(3):
                    for h in range(2):
                        base = n192 * h
                        v = [prod[base + 48 * d:base + 48 * (d + 1), 128 * q:128 * (q + 1)] for d in range(4)]
                        for k, w in enumerate(transpose4(v)):
                            i = RES * o + 4 * q + k
                            lhs2[48 * i:48 * (i + 1), pl.ds(pl.multiple_of(256 * g + 128 * h, 128), 128)] = w.astype(BF16)
            return c2

        lax.fori_loop(0, 4, outer, 0)
        for c in range(3):
            res = dot(lhs2[384 * c:384 * (c + 1), :], wo_p[...])
            for k in range(8):
                i = 8 * c + k
                for jg in range(6):
                    rt[pl.ds(8 * jg * UNIT + i, 8, stride=UNIT), :] = res[48 * k + 8 * jg:48 * k + 8 * jg + 8, :]
        own = rt[0:RES * UNIT, :].astype(BF16)

        @pl.when(home == dap)
        def _():
            r_recv[zz % 2, dap, unit] = own

        for r in (2, 1, 3):
            r_send[t, r] = rt[RES * UNIT * r:RES * UNIT * (r + 1), :].astype(BF16)
            r_copy(t, r, unit).start()

        @pl.when(home != dap)
        def _():
            r_send[t, 0] = own
            r_copy(t, 0, unit).start()
        return carry

    lax.fori_loop(0, 8, step, 0)

    for dy in range(4):
        for dx in range(4):
            pos = ((yy + 4 - dy) % 4) * 4 + (xx + 4 - dx) % 4
            mask_all[pl.ds(pl.multiple_of(16 * pos, 16), 16), :] = jnp.concatenate(
                [a_buf[dy * 4 + dx, p, AROWS:PROWS, :] for p in range(NP)], axis=1)
    ro, co = iota((256, 256), 0), iota((256, 256), 1)
    squeeze = jnp.where((ro < 192) & ((ro // RES) * 16 + ro % RES == co), 1.0, 0.0).astype(BF16)
    mask_rows = dot(squeeze, mask_all[...]).astype(BF16)
    for r in range(4):
        mask_cols = jnp.concatenate([b_buf[r, p, AROWS:PROWS, :] for p in range(NP)], axis=1)
        part = dot(mask_cols, mask_rows, NT)
        if r:
            n_send[r] = part
            n_copy(r).start()
        else:
            @pl.when(home == dap)
            def _(part=part):
                n_recv[zz % 2, dap] = part

            @pl.when(home != dap)
            def _(part=part):
                n_send[0] = part
                n_copy(0).start()

    pltpu.make_async_copy(z_hbm, z_v, z_sem).wait()
    bo = bo_ref[...].astype(F32)

    def arrive(ref, sem, src):
        pltpu.make_async_remote_copy(
            src_ref=src, dst_ref=ref, send_sem=n_ss.at[0], recv_sem=sem,
            device_id=dev(col, other), device_id_type=MESH).wait_recv()

    for k in range(2):
        for c in range(2):
            @pl.when(jnp.logical_not((zz == 2 * dap + k) & (dap == c)))
            def _(k=k, c=c):
                arrive(n_recv.at[k, c], n_rs.at[k, c], n_send.at[0])
        inv = 1.0 / (1e-3 + (n_recv[k, 0] + n_recv[k, 1]))
        inv_v[k] = inv.T

    for k in range(2):
        def finish(u, carry, k=k):
            for c in range(2):
                @pl.when(jnp.logical_not((zz == 2 * dap + k) & (dap == c)))
                def _(c=c):
                    arrive(r_recv.at[k, c, u], r_rs.at[k, c, u], r_send.at[0, 0])
            rows = pl.ds(pl.multiple_of(UNIT * u, 8), UNIT)
            dst = pl.ds(pl.multiple_of(192 * k + UNIT * u, 8), UNIT)
            inv = inv_v[k, rows, :]
            total = r_recv[k, 0, u].astype(F32) + r_recv[k, 1, u].astype(F32) + bo
            for j in range(RES):
                out_v[j, dst, :] = z_v[j, dst, :] + total[UNIT * j:UNIT * (j + 1), :] * inv[:, j:j + 1]
            return carry

        lax.fori_loop(0, 8, finish, 0)
        half = pl.ds(192 * k, 192)
        pltpu.make_async_copy(out_v.at[:, half, :], out_hbm.at[:, half, :], o_sem.at[k]).start()

    for slot, p, way in a_sent:
        a_copy(slot, p, way).wait_send()
    for r, p, way in b_sent:
        b_copy(r, p, way).wait_send()

    def left(t, carry):
        for r in (1, 2, 3):
            r_copy(t, r, 0).wait_send()

        @pl.when(home != dap)
        def _():
            r_copy(t, 0, 0).wait_send()
        return carry

    lax.fori_loop(0, 8, left, 0)
    for r in (1, 2, 3):
        n_copy(r).wait_send()

    @pl.when(home != dap)
    def _():
        n_copy(0).wait_send()

    for k in range(2):
        half = pl.ds(192 * k, 192)
        pltpu.make_async_copy(out_v.at[:, half, :], out_hbm.at[:, half, :], o_sem.at[k]).wait()


def solution(mesh):
    row_spec = P(("data", "dap"), "col", None)
    mask_spec = P(("data", "dap"), "col")
    in_specs = (row_spec, mask_spec, row_spec) + (P(),) * 8
    any_spec = pl.BlockSpec(memory_space=pl.ANY)
    vmem = pl.BlockSpec(memory_space=pltpu.VMEM)
    dma = pltpu.SemaphoreType.DMA
    scratch = [
        pltpu.VMEM((NP, RES, PIECE, CH), BF16),
        pltpu.VMEM((16, SEQ), F32),
        pltpu.VMEM((128, 4 * CH), BF16),
        pltpu.VMEM((AROWS, PIECE), F32),
        pltpu.VMEM((16, NP, PROWS, 128), BF16),
        pltpu.VMEM((4, NP, PROWS, 128), BF16),
        pltpu.VMEM((4 * AROWS, SEQ), BF16),
        pltpu.VMEM((UNIT * 48, HID * HID), BF16),
        pltpu.VMEM((48 * UNIT, PAIR), F32),
        pltpu.VMEM((HID * HID, PAIR), F32),
        pltpu.VMEM((HID * HID, PAIR), BF16),
        pltpu.VMEM((8, 4, RES * UNIT, PAIR), BF16),
        pltpu.VMEM((2, 2, 8, RES * UNIT, PAIR), BF16),
        pltpu.VMEM((4, 16, 256), F32),
        pltpu.VMEM((2, 2, 16, 256), F32),
        pltpu.VMEM((256, SEQ), BF16),
        pltpu.VMEM((2, 256, 16), F32),
        pltpu.VMEM((RES, 384, PAIR), F32),
        pltpu.VMEM((RES, 384, PAIR), F32),
        dma((NP,)), dma, dma((2,)),
        dma((16, NP, 4)), dma((16, NP)), dma((4, NP, 2)), dma((4, NP)),
        dma((8, 4)), dma((2, 2, 8)), dma((4,)), dma((2, 2)),
    ]

    def local_fn(m, mask, z, gamma, beta, w_a, b_a, w_b, b_b, w_out, b_out):
        out = pl.pallas_call(
            kernel,
            out_shape=jax.ShapeDtypeStruct((RES, 384, PAIR), F32),
            in_specs=[any_spec, vmem, any_spec] + [vmem] * 8,
            out_specs=any_spec,
            scratch_shapes=scratch,
            compiler_params=pltpu.CompilerParams(
                collective_id=0, has_side_effects=True, vmem_limit_bytes=60 * 1024 * 1024),
            name="opm",
        )(jnp.transpose(m, (1, 0, 2)), mask.T, jnp.transpose(z, (1, 0, 2)), gamma.reshape(1, CH), beta.reshape(1, CH),
          w_a.T, b_a.reshape(1, HID), w_b.T, b_b.reshape(1, HID), w_out, b_out.reshape(1, PAIR))
        return jnp.transpose(out, (1, 0, 2))

    return jax.shard_map(local_fn, mesh=mesh, in_specs=in_specs, out_specs=row_spec, check_vma=False)
```

time: 306 us -> 99.8 us (0.33)
  blocking collectives: 165 us -> 0 us
  Pallas kernels: 0 us -> 94 us
  matrix products: 80 us -> 0 us
  waiting for transfers between devices: 32.4 us -> 0 us
  between operations: 15 us -> 0.01 us
  other arithmetic: 10.9 us -> 0 us
    all_gather x1 -> x0, blocking collectives: 165 us -> none  [local_fn(): full_mask = lax.all_gather(mask_bf, 'col', axis=1, tiled=True)]
    pallas_call x0 -> x1, Pallas kernels: none -> 94 us  [local_fn(): pl.pallas_call(kernel, out_shape=jax.ShapeDtypeStruct((RES, 384, PAIR), F...]
    dot_general x5 -> x0, matrix products: 80 us -> none  [the longest x1 51.8 us: local_fn(): jnp.einsum('sic,scjz->ijz', full_a, proj_bw, preferred_element_type=jnp.f...]
    reduce_scatter x2 -> x0, waiting for transfers between devices: 32.4 us -> none  [the longest x1 32.4 us: local_fn(): row_sum = lax.psum_scatter(part_sum, 'dap', scatter_dimension=0, tiled=True)]
    reduce_sum x2 -> x0, other arithmetic: 6.19 us -> none  [the longest x1 3.27 us: layer_norm(): variance = jnp.mean(centred * centred, axis=-1, keepdims=True)]
    add x2 -> x0, other arithmetic: 3.96 us -> none  [the longest x1 3.07 us: local_fn(): pair_act + (row_sum + b_out.astype(jnp.float32)) / (0.001 + row_norm)[:,...]
  transfers between devices with their start and end apart: 3 -> 0, of which waited for: 1 -> 0; matrix products, arithmetic and copies ran while one was open for 26% -> 0% of each run, Pallas kernels for 0% -> 0%
where the time goes in v1:
time: 99.8 us; the launch traced here: 99.6 us
  Pallas kernels  94 us (94%)
  local copies, waits for them, and re-layouts  5.61 us (6%)
    pallas_call x1, Pallas kernels, local_fn(): pl.pallas_call(kernel, out_shape=jax.ShapeDtypeStruct((RES, 384, PAIR), F...  94 us
    unnamed x1, local copies, waits for them, and re-layouts  3.22 us

profile of v1, /device:TPU:1, one launch (start us, length us, event | category | flops | bytes accessed | tf_op | source)
XLA Modules:
  0.0 99.6 jit_solution(12747306126715234622)
XLA Ops:
  0.0 1.2 %reshape.15.gamma_ref = bf16[1,256]{1,0:T(2,128)(2,1)} reshape(bf16[256]{0:T(256)(128)(2,1)} %param.14) | data formatting | bytes 1024 | tf_op jit(solution)/shard_map/reshape | solution.py:436
  1.2 1.2 %reshape.16.beta_ref = bf16[1,256]{1,0:T(2,128)(2,1)} reshape(bf16[256]{0:T(256)(128)(2,1)} %param.15) | data formatting | bytes 1024 | tf_op jit(solution)/shard_map/reshape | solution.py:436
  2.4 94.0 %opm.1 = f32[12,384,128]{2,1,0:T(8,128)} custom-call(bf16[12,512,256]{2,1,0:T(8,128)(2,1)} %bitcast.10, s32[12,512]{1,0:T(8,128)} %bitcast.12, f32[12,384,128]{2,1,0:T(8,128)} %bitcast.11, bf16[1,256]{1,0:T(2,128)(2,1)} %reshape.15.gamma_ref, bf16[1,256]{1,0:T(2,128)(2,1)} %reshape.16.beta_ref, bf16[32,256]{1,0:T(8,128)(2,1)} %bitcast.13, ...), custom_call_target="tpu_custom_call" | custom-call | tf_op jit(solution)/shard_map/opm/pallas_call | solution.py:427
  96.4 3.2 %copy.13 = f32[384,12,128]{2,0,1:T(8,128)} copy(f32[384,12,128]{2,0,1:T(8,128)} %bitcast.9) | data formatting | bytes 4718592

commit v2 on v1

v2 whole, which is shorter than its diff:
```python
import jax
import jax.numpy as jnp
from jax import lax
from jax.experimental import pallas as pl
from jax.experimental.pallas import tpu as pltpu
from jax.sharding import PartitionSpec as P

F32 = jnp.float32
BF16 = jnp.bfloat16
MESH = pl.DeviceIdType.MESH
NT = (((1,), (1,)), ((), ()))

SEQ, RES, CH, HID, PAIR = 512, 12, 256, 32, 128
PIECE = 128
NP = SEQ // PIECE
AROWS = RES * HID
PROWS = AROWS + 16
UNIT = 2 * RES

WAYS = ("x+", "x-", "y+", "y-", "z+", "z-")
MOVE = {"x+": (0, 0, 1), "x-": (0, 0, -1), "y+": (0, 1, 0), "y-": (0, -1, 0), "z+": (1, 0, 0), "z-": (-1, 0, 0)}
STEPS = ((0, 0), (0, 1), (1, 0), (3, 0), (3, 1), (1, 1), (2, 0), (2, 1))
THIRDS = 3


def onward(place, p):
    dz, dy, dx = place
    plus = p < 2

    def along(d, axis):
        return [axis + "+"] if d == 1 and plus else [axis + "-"] if d == 3 and not plus else []

    if dz:
        return along(dz, "z")
    first, second, d1, d2 = ("x", "y", dx, dy) if p % 2 == 0 else ("y", "x", dy, dx)
    if d2:
        return along(d2, second)
    return along(d1, first) + [second + "+", second + "-"]


def relay_order(piece=2.22, hop=2.3, out=2.37, start=3.0, norm=1.3, regroup=1.6, product=2.6, issue=0.05):
    link = dict.fromkeys(WAYS, 0.0)
    here, sent, order = {}, set(), {}
    now, at = 0.0, (-1, 0)

    def send(place, p, way):
        link[way] = max(link[way], now) + piece
        here[tuple((a + b) % 4 for a, b in zip(place, MOVE[way])), p] = link[way] + hop

    def relay():
        nonlocal now
        for (place, p), _ in sorted(((k, v) for k, v in here.items() if v <= now and k not in sent), key=lambda kv: kv[1]):
            sent.add((place, p))
            for way in onward(place, p):
                send(place, p, way)
                order.setdefault(at, []).append((place, p, way))
                now += issue

    def ready(blocks):
        return all(here.get((b, p), now + 1) <= now for b in blocks for p in range(NP) if any(b))

    for p in range(NP):
        now = start + norm * p
        for way in WAYS:
            send((0, 0, 0), p, way)
    now += norm / 3
    todo = [("b", [(d, 0, 0) for d in (1, 2, 3)])]
    todo += [(i, [(0, dy, 2 * far), (0, dy, 1 + 2 * far)]) for i, (dy, far) in enumerate(STEPS)]
    for what, blocks in todo:
        relay()
        while not ready(blocks):
            now = min(v for v in here.values() if v > now)
            relay()
        if what == "b":
            now += regroup
        else:
            for third in range(THIRDS):
                at = (what, third)
                relay()
                now += product / THIRDS
        at = (0 if what == "b" else what + 1, 0)
    return order


def iota(shape, axis):
    return lax.broadcasted_iota(jnp.int32, shape, axis)


def dot(a, b, dims=None):
    if dims is None:
        return jnp.dot(a, b, preferred_element_type=F32)
    return lax.dot_general(a, b, dims, preferred_element_type=F32)


def kernel(m_hbm, mask_ref, z_hbm, gamma_ref, beta_ref, wa_ref, ba_ref, wb_ref, bb_ref, wo_ref, bo_ref,
           out_ref,
           m_v, mask_v, wabig, b32, a_buf, b_buf, bt, lhs2, rt, w32, wo_p, r_send, r_recv, n_send, n_recv,
           mask_all, inv_v, z_v,
           m_sem, z_sem, a_ss, a_rs, b_ss, b_rs, r_ss, r_rs, n_ss, n_rs):
    col = lax.axis_index("col")
    dap = lax.axis_index("dap")
    zz, yy, xx = col // 16, (col // 4) % 4, col % 4
    home = zz // 2
    other = 1 - dap

    def at(dz=0, dy=0, dx=0):
        return ((zz + dz) % 4) * 16 + ((yy + dy) % 4) * 4 + (xx + dx) % 4

    def dev(c, d):
        return {"col": c, "dap": d}

    for p in range(NP):
        pltpu.make_async_copy(m_hbm.at[:, pl.ds(PIECE * p, PIECE), :], m_v.at[p], m_sem.at[p]).start()
    barrier = pltpu.get_barrier_semaphore()
    greet = [dev(at(dy=1), dap), dev(at(dy=3), dap), dev(at(dx=1), dap), dev(at(dx=3), dap), dev(col, other)]
    for r in (1, 2, 3):
        for d in (0, 1):
            greet.append(dev(at(dz=r), d))
    for who in greet:
        pl.semaphore_signal(barrier, inc=1, device_id=who, device_id_type=MESH)

    mask_v[...] = jnp.zeros_like(mask_v)
    mask_v[0:RES, :] = mask_ref[...].astype(F32)
    wa = wa_ref[...]
    for k in range(4):
        rows = [wa if kk == k else jnp.zeros_like(wa) for kk in range(4)]
        wabig[:, CH * k:CH * (k + 1)] = jnp.concatenate(rows, axis=0)
    gamma = gamma_ref[...].astype(F32).reshape(1, CH)
    beta = beta_ref[...].astype(F32).reshape(1, CH)
    tile4 = jnp.where(iota((HID, 128), 1) % HID == iota((HID, 128), 0), 1.0, 0.0).astype(BF16)
    ba_row = dot(jnp.broadcast_to(ba_ref[...], (16, HID)), tile4)[0:1, :]
    eye = iota((HID, HID), 0) == iota((HID, HID), 1)
    bb_diag = jnp.where(eye, jnp.broadcast_to(bb_ref[...], (HID, HID)).astype(F32), 0.0).astype(BF16)
    bb_col = dot(bb_diag, jnp.ones((HID, 128), BF16))

    def hop(place, p, way):
        to = tuple((d + s) % 4 for d, s in zip(place, MOVE[way]))
        w = WAYS.index(way) % 4 % 2 + 2 * (way[0] == "y")
        if way[0] == "z":
            return pltpu.make_async_remote_copy(
                src_ref=b_buf.at[place[0], p], dst_ref=b_buf.at[to[0], p], send_sem=b_ss.at[place[0], p, w],
                recv_sem=b_rs.at[to[0], p], device_id=dev(at(*MOVE[way]), dap), device_id_type=MESH)
        src, dst = place[1] * 4 + place[2], to[1] * 4 + to[2]
        return pltpu.make_async_remote_copy(
            src_ref=a_buf.at[src, p], dst_ref=a_buf.at[dst, p], send_sem=a_ss.at[src, p, w],
            recv_sem=a_rs.at[dst, p], device_id=dev(at(*MOVE[way]), dap), device_id_type=MESH)

    def wait_a(i, p):
        pltpu.make_async_remote_copy(
            src_ref=a_buf.at[i, p], dst_ref=a_buf.at[i, p], send_sem=a_ss.at[i, p, 0], recv_sem=a_rs.at[i, p],
            device_id=dev(at(dx=1), dap), device_id_type=MESH).wait_recv()

    def wait_b(r, p):
        pltpu.make_async_remote_copy(
            src_ref=b_buf.at[r, p], dst_ref=b_buf.at[r, p], send_sem=b_ss.at[r, p, 0], recv_sem=b_rs.at[r, p],
            device_id=dev(at(dz=1), dap), device_id_type=MESH).wait_recv()

    hops = relay_order()
    sent = [((0, 0, 0), p, way) for p in range(NP) for way in WAYS]
    seen = set()

    def run(key):
        for place, p, way in hops.get(key, ()):
            if (place, p) not in seen:
                seen.add((place, p))
                if place[0]:
                    wait_b(place[0], p)
                else:
                    wait_a(place[1] * 4 + place[2], p)
            hop(place, p, way).start()
            sent.append((place, p, way))

    def project(p, carry):
        pltpu.make_async_copy(m_hbm.at[:, pl.ds(0, PIECE), :], m_v.at[p], m_sem.at[p]).wait()
        lanes = pl.ds(pl.multiple_of(PIECE * p, PIECE), PIECE)
        mask_p = mask_v[:, lanes]
        mask_b = mask_p.astype(BF16)
        mask_t = mask_p.T.astype(BF16)
        for q in range(3):
            xs = []
            for k in range(4):
                n = 4 * q + k
                v = m_v[p, n].astype(F32)
                mean = jnp.sum(v, axis=1, keepdims=True) * (1.0 / CH)
                cen = v - mean
                var = jnp.sum(cen * cen, axis=1, keepdims=True) * (1.0 / CH)
                x = (cen * lax.rsqrt(var + 1e-5) * gamma + beta).astype(BF16)
                xs.append(x)
                lin_b = dot(wb_ref[...], x, NT)
                b32[pl.ds(n, HID, stride=RES), :] = (lin_b + bb_col) * mask_p[n:n + 1, :]
            lin_a = dot(jnp.concatenate(xs, axis=1), wabig[...], NT)
            spread = jnp.where(iota((16, 128), 1) // HID + 4 * q == iota((16, 128), 0), 1.0, 0.0).astype(BF16)
            a_buf[0, p, 128 * q:128 * (q + 1), :] = ((lin_a + ba_row) * dot(mask_t, spread)).astype(BF16)
        a_buf[0, p, AROWS:PROWS, :] = mask_b
        b_buf[0, p, 0:AROWS, :] = b32[...].astype(BF16)
        b_buf[0, p, AROWS:PROWS, :] = mask_b

        @pl.when(p == 0)
        def _():
            pl.semaphore_wait(barrier, len(greet))

        for way in WAYS[4:] + WAYS[:4]:
            hop((0, 0, 0), p, way).start()
        return carry

    lax.fori_loop(0, NP, project, 0)
    pltpu.make_async_copy(z_hbm, z_v, z_sem).start()

    w32[...] = wo_ref[...].astype(F32)

    def order(d, carry):
        wo_p[pl.ds(pl.multiple_of(HID * d, HID), HID), :] = w32[pl.ds(d, HID, stride=HID), :].astype(BF16)
        return carry

    lax.fori_loop(0, HID, order, 0)

    run((-1, 0))

    for r in (1, 3, 2):
        for p in range(NP):
            if ((r, 0, 0), p) not in seen:
                wait_b(r, p)
    n192 = 4 * 4 * RES
    ro, co = iota((n192, n192), 0), iota((n192, n192), 1)
    want = ((ro // RES) % 4) * 48 + (ro // 48) * RES + ro % RES
    perm = jnp.where(want == co, 1.0, 0.0).astype(BF16)

    def regroup(g, carry):
        rows = pl.ds(pl.multiple_of(48 * g, 16), 48)
        cat = jnp.concatenate(
            [jnp.concatenate([b_buf[r, p, rows, :] for p in range(NP)], axis=1) for r in range(4)], axis=0)
        bt[pl.ds(pl.multiple_of(n192 * g, 64), n192), :] = dot(perm, cat).astype(BF16)
        return carry

    lax.fori_loop(0, 8, regroup, 0)

    lane = iota((1, 128), 1)
    low = lane < 64
    odd = (lane // HID) % 2 == 1

    def transpose4(v):
        def swap(u, w):
            t = pltpu.roll(jnp.where(low, w, u), 64, 1)
            return jnp.where(low, u, t), jnp.where(low, t, w)

        def swap2(u, w):
            return (jnp.where(odd, pltpu.roll(w, 32, 1), u), jnp.where(odd, w, pltpu.roll(u, 96, 1)))

        e0, e2 = swap(v[0], v[2])
        e1, e3 = swap(v[1], v[3])
        w0, w1 = swap2(e0, e1)
        w2, w3 = swap2(e2, e3)
        return w0, w1, w2, w3

    def r_copy(t, r, unit):
        return pltpu.make_async_remote_copy(
            src_ref=r_send.at[t, r], dst_ref=r_recv.at[zz % 2, dap, unit], send_sem=r_ss.at[t, r],
            recv_sem=r_rs.at[zz % 2, dap, unit], device_id=dev(at(dz=-r), home), device_id_type=MESH)

    def n_copy(r):
        return pltpu.make_async_remote_copy(
            src_ref=n_send.at[r], dst_ref=n_recv.at[zz % 2, dap], send_sem=n_ss.at[r],
            recv_sem=n_rs.at[zz % 2, dap], device_id=dev(at(dz=-r), home), device_id_type=MESH)

    def count():
        for dy in range(4):
            for dx in range(4):
                pos = ((yy + 4 - dy) % 4) * 4 + (xx + 4 - dx) % 4
                mask_all[pl.ds(pl.multiple_of(16 * pos, 16), 16), :] = jnp.concatenate(
                    [a_buf[dy * 4 + dx, p, AROWS:PROWS, :] for p in range(NP)], axis=1)
        ro, co = iota((256, 256), 0), iota((256, 256), 1)
        squeeze = jnp.where((ro < 192) & ((ro // RES) * 16 + ro % RES == co), 1.0, 0.0).astype(BF16)
        mask_rows = dot(squeeze, mask_all[...]).astype(BF16)
        for r in range(4):
            mask_cols = jnp.concatenate([b_buf[r, p, AROWS:PROWS, :] for p in range(NP)], axis=1)
            part = dot(mask_cols, mask_rows, NT)
            if r:
                n_send[r] = part
                n_copy(r).start()
            else:
                @pl.when(home == dap)
                def _(part=part):
                    n_recv[zz % 2, dap] = part

                @pl.when(home != dap)
                def _(part=part):
                    n_send[0] = part
                    n_copy(0).start()

    rest = {0: (), 1: (2,), 3: (0,), 2: (0, 2)}
    px = 3 - 2 * (xx % 2)

    def place(t):
        dy, far = jnp.int32(STEPS[7][0]), jnp.int32(STEPS[7][1])
        for i in range(6, -1, -1):
            dy = jnp.where(t == i, STEPS[i][0], dy)
            far = jnp.where(t == i, STEPS[i][1], far)
        pair = (xx // 2 + far) % 2
        return dy, pair, ((yy + 4 - dy) % 4) * 2 + pair

    def step(t, carry):
        for at_t in range(8):
            @pl.when(t == at_t)
            def _(at_t=at_t):
                run((at_t, 0))
                dy, far = STEPS[at_t]
                if not far:
                    for p in rest[dy]:
                        wait_a(dy * 4, p)
                    near, p = dy * 4 + px, 4 - px
                else:
                    for p in rest[dy] + (1, 3):
                        wait_a(dy * 4 + 2, p)
                    near, p = dy * 4 + 4 - px, px
                for q in rest[dy]:
                    wait_a(near, q)
                wait_a(near, p)
                if at_t == 7:
                    count()

        dy, pair, unit = place(t)
        slots = [dy * 4 + (xx + 4 - (2 * pair + o)) % 4 for o in range(2)]

        for c in range(THIRDS):
            for at_t in range(8):
                if c and (at_t, c) in hops:
                    @pl.when(t == at_t)
                    def _(at_t=at_t, c=c):
                        run((at_t, c))
            quads = (2 * c, 2 * c + 1)
            rhs = jnp.concatenate(
                [jnp.concatenate([a_buf[slots[q // 3], p, 128 * (q % 3):128 * (q % 3 + 1), :] for q in quads], axis=1)
                 for p in range(NP)], axis=0)
            for g in range(2):
                prod = dot(bt[4 * n192 * g:4 * n192 * (g + 1), :], rhs)
                for h in range(4):
                    for k2, q in enumerate(quads):
                        base = n192 * h
                        v = [prod[base + 48 * d:base + 48 * (d + 1), 128 * k2:128 * (k2 + 1)] for d in range(4)]
                        for k, w in enumerate(transpose4(v)):
                            i = 4 * q + k
                            lhs2[4 * g + h, 48 * i:48 * (i + 1), :] = w.astype(BF16)
        res = dot(jnp.concatenate([lhs2[g] for g in range(8)], axis=1), wo_p[...])
        for i in range(UNIT):
            for jg in range(6):
                rt[pl.ds(8 * jg * UNIT + i, 8, stride=UNIT), :] = res[48 * i + 8 * jg:48 * i + 8 * jg + 8, :]
        own = rt[0:RES * UNIT, :].astype(BF16)

        @pl.when(home == dap)
        def _():
            r_recv[zz % 2, dap, unit] = own

        for r in (2, 1, 3):
            r_send[t, r] = rt[RES * UNIT * r:RES * UNIT * (r + 1), :].astype(BF16)
            r_copy(t, r, unit).start()

        @pl.when(home != dap)
        def _():
            r_send[t, 0] = own
            r_copy(t, 0, unit).start()
        return carry

    lax.fori_loop(0, 8, step, 0)

    pltpu.make_async_copy(z_hbm, z_v, z_sem).wait()
    bo = bo_ref[...].astype(F32)

    def arrive(ref, sem, src):
        pltpu.make_async_remote_copy(
            src_ref=src, dst_ref=ref, send_sem=n_ss.at[0], recv_sem=sem,
            device_id=dev(col, other), device_id_type=MESH).wait_recv()

    for k in range(2):
        for c in range(2):
            @pl.when(jnp.logical_not((zz == 2 * dap + k) & (dap == c)))
            def _(k=k, c=c):
                arrive(n_recv.at[k, c], n_rs.at[k, c], n_send.at[0])
        inv = 1.0 / (1e-3 + (n_recv[k, 0] + n_recv[k, 1]))
        inv_v[k] = inv.T

    def finish(t, carry):
        _, _, u = place(t)
        for k in range(2):
            for c in range(2):
                @pl.when(jnp.logical_not((zz == 2 * dap + k) & (dap == c)))
                def _(k=k, c=c):
                    arrive(r_recv.at[k, c, u], r_rs.at[k, c, u], r_send.at[0, 0])
            rows = pl.ds(pl.multiple_of(UNIT * u, 8), UNIT)
            dst = pl.ds(pl.multiple_of(192 * k + UNIT * u, 8), UNIT)
            inv = inv_v[k, rows, :]
            total = r_recv[k, 0, u].astype(F32) + r_recv[k, 1, u].astype(F32) + bo
            for j in range(RES):
                out_ref[j, dst, :] = z_v[j, dst, :] + total[UNIT * j:UNIT * (j + 1), :] * inv[:, j:j + 1]
        return carry

    lax.fori_loop(0, 8, finish, 0)

    for place, p, way in sent:
        hop(place, p, way).wait_send()

    def left(t, carry):
        for r in (1, 2, 3):
            r_copy(t, r, 0).wait_send()

        @pl.when(home != dap)
        def _():
            r_copy(t, 0, 0).wait_send()
        return carry

    lax.fori_loop(0, 8, left, 0)
    for r in (1, 2, 3):
        n_copy(r).wait_send()

    @pl.when(home != dap)
    def _():
        n_copy(0).wait_send()


def solution(mesh):
    row_spec = P(("data", "dap"), "col", None)
    mask_spec = P(("data", "dap"), "col")
    in_specs = (row_spec, mask_spec, row_spec) + (P(),) * 8
    any_spec = pl.BlockSpec(memory_space=pl.ANY)
    vmem = pl.BlockSpec(memory_space=pltpu.VMEM)
    dma = pltpu.SemaphoreType.DMA
    scratch = [
        pltpu.VMEM((NP, RES, PIECE, CH), BF16),
        pltpu.VMEM((16, SEQ), F32),
        pltpu.VMEM((128, 4 * CH), BF16),
        pltpu.VMEM((AROWS, PIECE), F32),
        pltpu.VMEM((16, NP, PROWS, 128), BF16),
        pltpu.VMEM((4, NP, PROWS, 128), BF16),
        pltpu.VMEM((4 * AROWS, SEQ), BF16),
        pltpu.VMEM((8, UNIT * 48, 128), BF16),
        pltpu.VMEM((48 * UNIT, PAIR), F32),
        pltpu.VMEM((HID * HID, PAIR), F32),
        pltpu.VMEM((HID * HID, PAIR), BF16),
        pltpu.VMEM((8, 4, RES * UNIT, PAIR), BF16),
        pltpu.VMEM((2, 2, 8, RES * UNIT, PAIR), BF16),
        pltpu.VMEM((4, 16, 256), F32),
        pltpu.VMEM((2, 2, 16, 256), F32),
        pltpu.VMEM((256, SEQ), BF16),
        pltpu.VMEM((2, 256, 16), F32),
        pltpu.VMEM((RES, 384, PAIR), F32),
        dma((NP,)), dma,
        dma((16, NP, 4)), dma((16, NP)), dma((4, NP, 2)), dma((4, NP)),
        dma((8, 4)), dma((2, 2, 8)), dma((4,)), dma((2, 2)),
    ]

    def local_fn(m, mask, z, gamma, beta, w_a, b_a, w_b, b_b, w_out, b_out):
        out = pl.pallas_call(
            kernel,
            out_shape=pltpu.VMEM((RES, 384, PAIR), F32),
            in_specs=[any_spec, vmem, any_spec] + [vmem] * 8,
            out_specs=vmem,
            scratch_shapes=scratch,
            compiler_params=pltpu.CompilerParams(
                collective_id=0, has_side_effects=True, vmem_limit_bytes=60 * 1024 * 1024),
            name="opm",
        )(jnp.transpose(m, (1, 0, 2)), mask.T, jnp.transpose(z, (1, 0, 2)), gamma, beta,
          w_a.T, b_a.reshape(1, HID), w_b.T, b_b.reshape(1, HID), w_out, b_out.reshape(1, PAIR))
        return jnp.transpose(out, (1, 0, 2))

    return jax.shard_map(local_fn, mesh=mesh, in_specs=in_specs, out_specs=row_spec, check_vma=False)
```

time: 99.8 us -> 65.1 us (0.65)
  Pallas kernels: 94 us -> 63.5 us
  local copies, waits for them, and re-layouts: 5.61 us -> 1.41 us
    pallas_call x1, Pallas kernels: 94 us -> 63.5 us  [local_fn(): pl.pallas_call(kernel, out_shape=pltpu.VMEM((RES, 384, PAIR), F32), in_sp...]
    reshape x2 -> x0, local copies, waits for them, and re-layouts: 2.39 us -> none  [the longest x1 1.22 us: local_fn(): gamma.reshape(1, CH)]
    unnamed x1, local copies, waits for them, and re-layouts: 3.22 us -> 1.41 us
where the time goes in v2:
time: 65.1 us; the launch traced here: 65 us
  Pallas kernels  63.5 us (98%)
  local copies, waits for them, and re-layouts  1.41 us (2%)
    pallas_call x1, Pallas kernels, local_fn(): pl.pallas_call(kernel, out_shape=pltpu.VMEM((RES, 384, PAIR), F32), in_sp...  63.5 us
    unnamed x1, local copies, waits for them, and re-layouts  1.41 us

profile of v2, /device:TPU:1, one launch (start us, length us, event | category | flops | bytes accessed | tf_op | source)
XLA Modules:
  0.0 65.0 jit_solution(3984467111264453231)
XLA Ops:
  0.0 63.5 %opm.1 = f32[12,384,128]{2,1,0:T(8,128)S(1)} custom-call(bf16[12,512,256]{2,1,0:T(8,128)(2,1)} %bitcast.10, s32[12,512]{1,0:T(8,128)} %bitcast.12, f32[12,384,128]{2,1,0:T(8,128)} %bitcast.11, bf16[256]{0:T(256)(128)(2,1)} %gamma_ref.1, bf16[256]{0:T(256)(128)(2,1)} %beta_ref.1, bf16[32,256]{1,0:T(8,128)(2,1)} %bitcast.13, bf16[1,32]{1,0:T(2,128)(2,1)} %bitcast.15, ...), custom_call_target="tpu_custom_call" | custom-call | tf_op jit(solution)/shard_map/opm/pallas_call | solution.py:451
  63.5 1.4 %copy.13 = f32[384,12,128]{2,0,1:T(8,128)} copy(f32[384,12,128]{2,0,1:T(8,128)S(1)} %bitcast.9) | data formatting | bytes 4718592

commit v3 on v2

--- a/solution.py
+++ b/solution.py
@@ -20,7 +20,6 @@
 WAYS = ("x+", "x-", "y+", "y-", "z+", "z-")
 MOVE = {"x+": (0, 0, 1), "x-": (0, 0, -1), "y+": (0, 1, 0), "y-": (0, -1, 0), "z+": (1, 0, 0), "z-": (-1, 0, 0)}
 STEPS = ((0, 0), (0, 1), (1, 0), (3, 0), (3, 1), (1, 1), (2, 0), (2, 1))
-THIRDS = 3
 
 
 def onward(place, p):
@@ -41,7 +40,7 @@
 def relay_order(piece=2.22, hop=2.3, out=2.37, start=3.0, norm=1.3, regroup=1.6, product=2.6, issue=0.05):
     link = dict.fromkeys(WAYS, 0.0)
     here, sent, order = {}, set(), {}
-    now, at = 0.0, (-1, 0)
+    now, at = 0.0, -1
 
     def send(place, p, way):
         link[way] = max(link[way], now) + piece
@@ -74,11 +73,8 @@
         if what == "b":
             now += regroup
         else:
-            for third in range(THIRDS):
-                at = (what, third)
-                relay()
-                now += product / THIRDS
-        at = (0 if what == "b" else what + 1, 0)
+            now += product
+        at = 0 if what == "b" else what + 1
     return order
 
 
@@ -214,7 +210,7 @@
 
     lax.fori_loop(0, HID, order, 0)
 
-    run((-1, 0))
+    run(-1)
 
     for r in (1, 3, 2):
         for p in range(NP):
@@ -302,7 +298,7 @@
         for at_t in range(8):
             @pl.when(t == at_t)
             def _(at_t=at_t):
-                run((at_t, 0))
+                run(at_t)
                 dy, far = STEPS[at_t]
                 if not far:
                     for p in rest[dy]:
@@ -321,12 +317,7 @@
         dy, pair, unit = place(t)
         slots = [dy * 4 + (xx + 4 - (2 * pair + o)) % 4 for o in range(2)]
 
-        for c in range(THIRDS):
-            for at_t in range(8):
-                if c and (at_t, c) in hops:
-                    @pl.when(t == at_t)
-                    def _(at_t=at_t, c=c):
-                        run((at_t, c))
+        for c in range(3):
             quads = (2 * c, 2 * c + 1)
             rhs = jnp.concatenate(
                 [jnp.concatenate([a_buf[slots[q // 3], p, 128 * (q % 3):128 * (q % 3 + 1), :] for q in quads], axis=1)

time: 65.1 us -> 64.2 us (0.986)
  Pallas kernels: 63.5 us -> 62.6 us
    pallas_call x1, Pallas kernels: 63.5 us -> 62.6 us  [local_fn(): pl.pallas_call(kernel, out_shape=pltpu.VMEM((RES, 384, PAIR), F32), in_sp...]
where the time goes in v3:
time: 64.2 us; the launch traced here: 64 us
  Pallas kernels  62.6 us (98%)
  local copies, waits for them, and re-layouts  1.41 us (2%)
    pallas_call x1, Pallas kernels, local_fn(): pl.pallas_call(kernel, out_shape=pltpu.VMEM((RES, 384, PAIR), F32), in_sp...  62.6 us
    unnamed x1, local copies, waits for them, and re-layouts  1.41 us

profile of v3, /device:TPU:1, one launch (start us, length us, event | category | flops | bytes accessed | tf_op | source)
XLA Modules:
  0.0 64.0 jit_solution(10267177216209947089)
XLA Ops:
  0.0 62.6 %opm.1 = f32[12,384,128]{2,1,0:T(8,128)S(1)} custom-call(bf16[12,512,256]{2,1,0:T(8,128)(2,1)} %bitcast.10, s32[12,512]{1,0:T(8,128)} %bitcast.12, f32[12,384,128]{2,1,0:T(8,128)} %bitcast.11, bf16[256]{0:T(256)(128)(2,1)} %gamma_ref.1, bf16[256]{0:T(256)(128)(2,1)} %beta_ref.1, bf16[32,256]{1,0:T(8,128)(2,1)} %bitcast.13, bf16[1,32]{1,0:T(2,128)(2,1)} %bitcast.15, ...), custom_call_target="tpu_custom_call" | custom-call | tf_op jit(solution)/shard_map/opm/pallas_call | solution.py:442
  62.6 1.4 %copy.13 = f32[384,12,128]{2,0,1:T(8,128)} copy(f32[384,12,128]{2,0,1:T(8,128)S(1)} %bitcast.9) | data formatting | bytes 4718592

commit v4 on v3

--- a/solution.py
+++ b/solution.py
@@ -19,7 +19,7 @@
 
 WAYS = ("x+", "x-", "y+", "y-", "z+", "z-")
 MOVE = {"x+": (0, 0, 1), "x-": (0, 0, -1), "y+": (0, 1, 0), "y-": (0, -1, 0), "z+": (1, 0, 0), "z-": (-1, 0, 0)}
-STEPS = ((0, 0), (0, 1), (1, 0), (3, 0), (3, 1), (1, 1), (2, 0), (2, 1))
+STEPS = ((0, 0), (0, 1), (1, 0), (3, 0), (1, 1), (3, 1), (2, 0), (2, 1))
 
 
 def onward(place, p):
@@ -37,45 +37,20 @@
     return along(d1, first) + [second + "+", second + "-"]
 
 
-def relay_order(piece=2.22, hop=2.3, out=2.37, start=3.0, norm=1.3, regroup=1.6, product=2.6, issue=0.05):
-    link = dict.fromkeys(WAYS, 0.0)
-    here, sent, order = {}, set(), {}
-    now, at = 0.0, -1
-
-    def send(place, p, way):
-        link[way] = max(link[way], now) + piece
-        here[tuple((a + b) % 4 for a, b in zip(place, MOVE[way])), p] = link[way] + hop
-
-    def relay():
-        nonlocal now
-        for (place, p), _ in sorted(((k, v) for k, v in here.items() if v <= now and k not in sent), key=lambda kv: kv[1]):
-            sent.add((place, p))
-            for way in onward(place, p):
-                send(place, p, way)
-                order.setdefault(at, []).append((place, p, way))
-                now += issue
-
-    def ready(blocks):
-        return all(here.get((b, p), now + 1) <= now for b in blocks for p in range(NP) if any(b))
-
-    for p in range(NP):
-        now = start + norm * p
-        for way in WAYS:
-            send((0, 0, 0), p, way)
-    now += norm / 3
-    todo = [("b", [(d, 0, 0) for d in (1, 2, 3)])]
-    todo += [(i, [(0, dy, 2 * far), (0, dy, 1 + 2 * far)]) for i, (dy, far) in enumerate(STEPS)]
-    for what, blocks in todo:
-        relay()
-        while not ready(blocks):
-            now = min(v for v in here.values() if v > now)
-            relay()
-        if what == "b":
-            now += regroup
-        else:
-            now += product
-        at = 0 if what == "b" else what + 1
-    return order
+def all_hops():
+    hops = [((0, 0, 0), p, way) for p in range(NP) for way in WAYS]
+    for place, p, way in hops:
+        to = tuple((a + b) % 4 for a, b in zip(place, MOVE[way]))
+        for h in ((to, p, w) for w in onward(to, p)):
+            if h not in hops:
+                hops.append(h)
+    return hops
+
+
+ORDER = {-5: (0, 1, 2, 3, 4, 5), -4: (6, 8, 10), -3: (12, 13, 14, 15, 16, 17), -2: (18, 19, 7, 20, 9, 21, 22, 23, 11),
+    -1: (24, 25, 26, 30, 27, 28, 31, 40, 34, 37, 33, 44, 41, 42, 45, 51, 35, 36, 38, 39, 46, 47, 32, 48, 49, 50, 61,
+    62), 0: (52, 53), 1: (58, 54, 63), 2: (59, 29, 60, 64), 3: (56, 65, 67, 66, 57, 55, 43, 70), 4: (68,), 6: (69,
+    71)}
 
 
 def iota(shape, axis):
@@ -88,11 +63,12 @@
     return lax.dot_general(a, b, dims, preferred_element_type=F32)
 
 
-def kernel(m_hbm, mask_ref, z_hbm, gamma_ref, beta_ref, wa_ref, ba_ref, wb_ref, bb_ref, wo_ref, bo_ref,
+def kernel(m_hbm, mask_hbm, z_hbm, gamma_hbm, beta_hbm, wa_hbm, ba_hbm, wb_hbm, bb_hbm, wo_hbm, bo_hbm,
            out_ref,
+           mask_ref, gamma_ref, beta_ref, wa_ref, ba_ref, wb_ref, bb_ref, wo_ref, bo_ref,
            m_v, mask_v, wabig, b32, a_buf, b_buf, bt, lhs2, rt, w32, wo_p, r_send, r_recv, n_send, n_recv,
            mask_all, inv_v, z_v,
-           m_sem, z_sem, a_ss, a_rs, b_ss, b_rs, r_ss, r_rs, n_ss, n_rs):
+           in_sem, m_sem, z_sem, a_ss, a_rs, b_ss, b_rs, r_ss, r_rs, n_ss, n_rs):
     col = lax.axis_index("col")
     dap = lax.axis_index("dap")
     zz, yy, xx = col // 16, (col // 4) % 4, col % 4
@@ -105,8 +81,14 @@
     def dev(c, d):
         return {"col": c, "dap": d}
 
+    small = [pltpu.make_async_copy(src, dst, in_sem.at[i]) for i, (src, dst) in enumerate((
+        (mask_hbm, mask_ref), (gamma_hbm, gamma_ref), (beta_hbm, beta_ref), (wa_hbm, wa_ref), (ba_hbm, ba_ref),
+        (wb_hbm, wb_ref), (bb_hbm, bb_ref), (wo_hbm, wo_ref), (bo_hbm, bo_ref)))]
     for p in range(NP):
         pltpu.make_async_copy(m_hbm.at[:, pl.ds(PIECE * p, PIECE), :], m_v.at[p], m_sem.at[p]).start()
+        if p == 0:
+            for copy in small:
+                copy.start()
     barrier = pltpu.get_barrier_semaphore()
     greet = [dev(at(dy=1), dap), dev(at(dy=3), dap), dev(at(dx=1), dap), dev(at(dx=3), dap), dev(col, other)]
     for r in (1, 2, 3):
@@ -115,6 +97,8 @@
     for who in greet:
         pl.semaphore_signal(barrier, inc=1, device_id=who, device_id_type=MESH)
 
+    for copy in small:
+        copy.wait()
     mask_v[...] = jnp.zeros_like(mask_v)
     mask_v[0:RES, :] = mask_ref[...].astype(F32)
     wa = wa_ref[...]
@@ -151,18 +135,21 @@
             src_ref=b_buf.at[r, p], dst_ref=b_buf.at[r, p], send_sem=b_ss.at[r, p, 0], recv_sem=b_rs.at[r, p],
             device_id=dev(at(dz=1), dap), device_id_type=MESH).wait_recv()
 
-    hops = relay_order()
-    sent = [((0, 0, 0), p, way) for p in range(NP) for way in WAYS]
-    seen = set()
+    hops = all_hops()
+    sent, seen = [], set()
+
+    def need(place, p):
+        if any(place) and (place, p) not in seen:
+            seen.add((place, p))
+            if place[0]:
+                wait_b(place[0], p)
+            else:
+                wait_a(place[1] * 4 + place[2], p)
 
     def run(key):
-        for place, p, way in hops.get(key, ()):
-            if (place, p) not in seen:
-                seen.add((place, p))
-                if place[0]:
-                    wait_b(place[0], p)
-                else:
-                    wait_a(place[1] * 4 + place[2], p)
+        for i in ORDER.get(key, ()):
+            place, p, way = hops[i]
+            need(place, p)
             hop(place, p, way).start()
             sent.append((place, p, way))
 
@@ -195,8 +182,10 @@
         def _():
             pl.semaphore_wait(barrier, len(greet))
 
-        for way in WAYS[4:] + WAYS[:4]:
-            hop((0, 0, 0), p, way).start()
+        for k in range(NP):
+            @pl.when(p == k)
+            def _(k=k):
+                run(k - 5)
         return carry
 
     lax.fori_loop(0, NP, project, 0)
@@ -214,21 +203,16 @@
 
     for r in (1, 3, 2):
         for p in range(NP):
-            if ((r, 0, 0), p) not in seen:
-                wait_b(r, p)
+            need((r, 0, 0), p)
     n192 = 4 * 4 * RES
     ro, co = iota((n192, n192), 0), iota((n192, n192), 1)
     want = ((ro // RES) % 4) * 48 + (ro // 48) * RES + ro % RES
     perm = jnp.where(want == co, 1.0, 0.0).astype(BF16)
 
-    def regroup(g, carry):
-        rows = pl.ds(pl.multiple_of(48 * g, 16), 48)
+    for g in range(8):
         cat = jnp.concatenate(
-            [jnp.concatenate([b_buf[r, p, rows, :] for p in range(NP)], axis=1) for r in range(4)], axis=0)
-        bt[pl.ds(pl.multiple_of(n192 * g, 64), n192), :] = dot(perm, cat).astype(BF16)
-        return carry
-
-    lax.fori_loop(0, 8, regroup, 0)
+            [jnp.concatenate([b_buf[r, p, 48 * g:48 * (g + 1), :] for p in range(NP)], axis=1) for r in range(4)], axis=0)
+        bt[n192 * g:n192 * (g + 1), :] = dot(perm, cat).astype(BF16)
 
     lane = iota((1, 128), 1)
     low = lane < 64
@@ -300,6 +284,10 @@
             def _(at_t=at_t):
                 run(at_t)
                 dy, far = STEPS[at_t]
+                for dx in (2 * far, 1, 3):
+                    for p in range(NP):
+                        if onward((0, dy, dx), p):
+                            need((0, dy, dx), p)
                 if not far:
                     for p in rest[dy]:
                         wait_a(dy * 4, p)
@@ -415,6 +403,9 @@
     vmem = pl.BlockSpec(memory_space=pltpu.VMEM)
     dma = pltpu.SemaphoreType.DMA
     scratch = [
+        pltpu.VMEM((RES, SEQ), jnp.int32), pltpu.VMEM((CH,), BF16), pltpu.VMEM((CH,), BF16), pltpu.VMEM((HID, CH), BF16),
+        pltpu.VMEM((1, HID), BF16), pltpu.VMEM((HID, CH), BF16), pltpu.VMEM((1, HID), BF16),
+        pltpu.VMEM((HID * HID, PAIR), BF16), pltpu.VMEM((1, PAIR), BF16),
         pltpu.VMEM((NP, RES, PIECE, CH), BF16),
         pltpu.VMEM((16, SEQ), F32),
         pltpu.VMEM((128, 4 * CH), BF16),
@@ -433,7 +424,7 @@
         pltpu.VMEM((256, SEQ), BF16),
         pltpu.VMEM((2, 256, 16), F32),
         pltpu.VMEM((RES, 384, PAIR), F32),
-        dma((NP,)), dma,
+        dma((9,)), dma((NP,)), dma,
         dma((16, NP, 4)), dma((16, NP)), dma((4, NP, 2)), dma((4, NP)),
         dma((8, 4)), dma((2, 2, 8)), dma((4,)), dma((2, 2)),
     ]
@@ -442,7 +433,7 @@
         out = pl.pallas_call(
             kernel,
             out_shape=pltpu.VMEM((RES, 384, PAIR), F32),
-            in_specs=[any_spec, vmem, any_spec] + [vmem] * 8,
+            in_specs=[any_spec] * 11,
             out_specs=vmem,
             scratch_shapes=scratch,
             compiler_params=pltpu.CompilerParams(

time: 64.2 us -> 59.5 us (0.927)
  Pallas kernels: 62.6 us -> 57.9 us
    pallas_call x1, Pallas kernels: 62.6 us -> 57.9 us  [local_fn(): pl.pallas_call(kernel, out_shape=pltpu.VMEM((RES, 384, PAIR), F32), in_sp...]
where the time goes in v4:
time: 59.5 us; the launch traced here: 59.4 us
  Pallas kernels  57.9 us (97%)
  local copies, waits for them, and re-layouts  1.41 us (2%)
    pallas_call x1, Pallas kernels, local_fn(): pl.pallas_call(kernel, out_shape=pltpu.VMEM((RES, 384, PAIR), F32), in_sp...  57.9 us
    unnamed x1, local copies, waits for them, and re-layouts  1.41 us

profile of v4, /device:TPU:1, one launch (start us, length us, event | category | flops | bytes accessed | tf_op | source)
XLA Modules:
  0.0 59.4 jit_solution(2386749255542421098)
XLA Ops:
  0.0 57.9 %opm.1 = f32[12,384,128]{2,1,0:T(8,128)S(1)} custom-call(bf16[12,512,256]{2,1,0:T(8,128)(2,1)} %bitcast.10, s32[12,512]{1,0:T(8,128)} %bitcast.12, f32[12,384,128]{2,1,0:T(8,128)} %bitcast.11, bf16[256]{0:T(256)(128)(2,1)} %gamma_hbm.1, bf16[256]{0:T(256)(128)(2,1)} %beta_hbm.1, bf16[32,256]{1,0:T(8,128)(2,1)} %bitcast.13, bf16[1,32]{1,0:T(2,128)(2,1)} %bitcast.15, ...), custom_call_target="tpu_custom_call" | custom-call | tf_op jit(solution)/shard_map/opm/pallas_call | solution.py:433
  57.9 1.4 %copy.13 = f32[384,12,128]{2,0,1:T(8,128)} copy(f32[384,12,128]{2,0,1:T(8,128)S(1)} %bitcast.9) | data formatting | bytes 4718592

commit v5 on v4

--- a/solution.py
+++ b/solution.py
@@ -11,6 +11,7 @@
 NT = (((1,), (1,)), ((), ()))
 
 SEQ, RES, CH, HID, PAIR = 512, 12, 256, 32, 128
+LANES = 128
 PIECE = 128
 NP = SEQ // PIECE
 AROWS = RES * HID
@@ -18,20 +19,24 @@
 UNIT = 2 * RES
 
 WAYS = ("x+", "x-", "y+", "y-", "z+", "z-")
-MOVE = {"x+": (0, 0, 1), "x-": (0, 0, -1), "y+": (0, 1, 0), "y-": (0, -1, 0), "z+": (1, 0, 0), "z-": (-1, 0, 0)}
+MOVE = {w: tuple((w[0] == ax) * (1 if w[1] == "+" else -1) for ax in "zyx") for w in WAYS}
 STEPS = ((0, 0), (0, 1), (1, 0), (3, 0), (1, 1), (3, 1), (2, 0), (2, 1))
+
+
+PLUS = {"x": (1, 2), "y": (2, 3), "z": (0, 1)}
 
 
 def onward(place, p):
     dz, dy, dx = place
-    plus = p < 2
 
     def along(d, axis):
-        return [axis + "+"] if d == 1 and plus else [axis + "-"] if d == 3 and not plus else []
+        if d == 1 and p in PLUS[axis]:
+            return [axis + "+"]
+        return [axis + "-"] if d == 3 and p not in PLUS[axis] else []
 
     if dz:
         return along(dz, "z")
-    first, second, d1, d2 = ("x", "y", dx, dy) if p % 2 == 0 else ("y", "x", dy, dx)
+    first, second, d1, d2 = ("y", "x", dy, dx) if p % 2 else ("x", "y", dx, dy)
     if d2:
         return along(d2, second)
     return along(d1, first) + [second + "+", second + "-"]
@@ -47,10 +52,9 @@
     return hops
 
 
-ORDER = {-5: (0, 1, 2, 3, 4, 5), -4: (6, 8, 10), -3: (12, 13, 14, 15, 16, 17), -2: (18, 19, 7, 20, 9, 21, 22, 23, 11),
-    -1: (24, 25, 26, 30, 27, 28, 31, 40, 34, 37, 33, 44, 41, 42, 45, 51, 35, 36, 38, 39, 46, 47, 32, 48, 49, 50, 61,
-    62), 0: (52, 53), 1: (58, 54, 63), 2: (59, 29, 60, 64), 3: (56, 65, 67, 66, 57, 55, 43, 70), 4: (68,), 6: (69,
-    71)}
+ORDER = {-5: (0, 1, 2, 3, 4, 5), -4: (6, 7, 8, 9, 10), -3: (17,), -2: (12, 19, 14, 15, 22, 23), -1: (18, 13, 20, 21,
+    16, 11, 26, 24, 28, 30, 31, 44, 32, 33, 27, 25, 37, 51, 38, 45, 39, 40, 47, 48, 41, 42, 49, 50, 46, 34), 1: (35,
+    36, 60, 61), 2: (56, 66, 53, 55, 43, 54), 3: (57, 65, 62, 29, 59, 67), 4: (64, 58, 63, 52), 5: (69, 71, 70, 68)}
 
 
 def iota(shape, axis):
@@ -107,36 +111,35 @@
         wabig[:, CH * k:CH * (k + 1)] = jnp.concatenate(rows, axis=0)
     gamma = gamma_ref[...].astype(F32).reshape(1, CH)
     beta = beta_ref[...].astype(F32).reshape(1, CH)
-    tile4 = jnp.where(iota((HID, 128), 1) % HID == iota((HID, 128), 0), 1.0, 0.0).astype(BF16)
+    tile4 = jnp.where(iota((HID, LANES), 1) % HID == iota((HID, LANES), 0), 1.0, 0.0).astype(BF16)
     ba_row = dot(jnp.broadcast_to(ba_ref[...], (16, HID)), tile4)[0:1, :]
     eye = iota((HID, HID), 0) == iota((HID, HID), 1)
     bb_diag = jnp.where(eye, jnp.broadcast_to(bb_ref[...], (HID, HID)).astype(F32), 0.0).astype(BF16)
-    bb_col = dot(bb_diag, jnp.ones((HID, 128), BF16))
+    bb_col = dot(bb_diag, jnp.ones((HID, LANES), BF16))
 
     def hop(place, p, way):
         to = tuple((d + s) % 4 for d, s in zip(place, MOVE[way]))
-        w = WAYS.index(way) % 4 % 2 + 2 * (way[0] == "y")
         if way[0] == "z":
             return pltpu.make_async_remote_copy(
-                src_ref=b_buf.at[place[0], p], dst_ref=b_buf.at[to[0], p], send_sem=b_ss.at[place[0], p, w],
+                src_ref=b_buf.at[place[0], p], dst_ref=b_buf.at[to[0], p], send_sem=b_ss,
                 recv_sem=b_rs.at[to[0], p], device_id=dev(at(*MOVE[way]), dap), device_id_type=MESH)
         src, dst = place[1] * 4 + place[2], to[1] * 4 + to[2]
         return pltpu.make_async_remote_copy(
-            src_ref=a_buf.at[src, p], dst_ref=a_buf.at[dst, p], send_sem=a_ss.at[src, p, w],
+            src_ref=a_buf.at[src, p], dst_ref=a_buf.at[dst, p], send_sem=a_ss,
             recv_sem=a_rs.at[dst, p], device_id=dev(at(*MOVE[way]), dap), device_id_type=MESH)
 
     def wait_a(i, p):
         pltpu.make_async_remote_copy(
-            src_ref=a_buf.at[i, p], dst_ref=a_buf.at[i, p], send_sem=a_ss.at[i, p, 0], recv_sem=a_rs.at[i, p],
+            src_ref=a_buf.at[i, p], dst_ref=a_buf.at[i, p], send_sem=a_ss, recv_sem=a_rs.at[i, p],
             device_id=dev(at(dx=1), dap), device_id_type=MESH).wait_recv()
 
     def wait_b(r, p):
         pltpu.make_async_remote_copy(
-            src_ref=b_buf.at[r, p], dst_ref=b_buf.at[r, p], send_sem=b_ss.at[r, p, 0], recv_sem=b_rs.at[r, p],
+            src_ref=b_buf.at[r, p], dst_ref=b_buf.at[r, p], send_sem=b_ss, recv_sem=b_rs.at[r, p],
             device_id=dev(at(dz=1), dap), device_id_type=MESH).wait_recv()
 
     hops = all_hops()
-    sent, seen = [], set()
+    seen = set()
 
     def need(place, p):
         if any(place) and (place, p) not in seen:
@@ -151,7 +154,6 @@
             place, p, way = hops[i]
             need(place, p)
             hop(place, p, way).start()
-            sent.append((place, p, way))
 
     def project(p, carry):
         pltpu.make_async_copy(m_hbm.at[:, pl.ds(0, PIECE), :], m_v.at[p], m_sem.at[p]).wait()
@@ -172,8 +174,8 @@
                 lin_b = dot(wb_ref[...], x, NT)
                 b32[pl.ds(n, HID, stride=RES), :] = (lin_b + bb_col) * mask_p[n:n + 1, :]
             lin_a = dot(jnp.concatenate(xs, axis=1), wabig[...], NT)
-            spread = jnp.where(iota((16, 128), 1) // HID + 4 * q == iota((16, 128), 0), 1.0, 0.0).astype(BF16)
-            a_buf[0, p, 128 * q:128 * (q + 1), :] = ((lin_a + ba_row) * dot(mask_t, spread)).astype(BF16)
+            spread = jnp.where(iota((16, LANES), 1) // HID + 4 * q == iota((16, LANES), 0), 1.0, 0.0).astype(BF16)
+            a_buf[0, p, LANES * q:LANES * (q + 1), :] = ((lin_a + ba_row) * dot(mask_t, spread)).astype(BF16)
         a_buf[0, p, AROWS:PROWS, :] = mask_b
         b_buf[0, p, 0:AROWS, :] = b32[...].astype(BF16)
         b_buf[0, p, AROWS:PROWS, :] = mask_b
@@ -214,7 +216,7 @@
             [jnp.concatenate([b_buf[r, p, 48 * g:48 * (g + 1), :] for p in range(NP)], axis=1) for r in range(4)], axis=0)
         bt[n192 * g:n192 * (g + 1), :] = dot(perm, cat).astype(BF16)
 
-    lane = iota((1, 128), 1)
+    lane = iota((1, LANES), 1)
     low = lane < 64
     odd = (lane // HID) % 2 == 1
 
@@ -234,12 +236,12 @@
 
     def r_copy(t, r, unit):
         return pltpu.make_async_remote_copy(
-            src_ref=r_send.at[t, r], dst_ref=r_recv.at[zz % 2, dap, unit], send_sem=r_ss.at[t, r],
+            src_ref=r_send.at[t, r], dst_ref=r_recv.at[zz % 2, dap, unit], send_sem=r_ss.at[1 if r else 0],
             recv_sem=r_rs.at[zz % 2, dap, unit], device_id=dev(at(dz=-r), home), device_id_type=MESH)
 
     def n_copy(r):
         return pltpu.make_async_remote_copy(
-            src_ref=n_send.at[r], dst_ref=n_recv.at[zz % 2, dap], send_sem=n_ss.at[r],
+            src_ref=n_send.at[r], dst_ref=n_recv.at[zz % 2, dap], send_sem=n_ss.at[1 if r else 0],
             recv_sem=n_rs.at[zz % 2, dap], device_id=dev(at(dz=-r), home), device_id_type=MESH)
 
     def count():
@@ -267,7 +269,7 @@
                     n_send[0] = part
                     n_copy(0).start()
 
-    rest = {0: (), 1: (2,), 3: (0,), 2: (0, 2)}
+    stay = [p for d in (1, 3) for p in (1, 3) if not onward((0, 1, d), p)]
     px = 3 - 2 * (xx % 2)
 
     def place(t):
@@ -284,21 +286,18 @@
             def _(at_t=at_t):
                 run(at_t)
                 dy, far = STEPS[at_t]
+                rest = [p for p in (0, 2) if dy and not onward((0, dy, 1), p)]
                 for dx in (2 * far, 1, 3):
                     for p in range(NP):
                         if onward((0, dy, dx), p):
                             need((0, dy, dx), p)
-                if not far:
-                    for p in rest[dy]:
-                        wait_a(dy * 4, p)
-                    near, p = dy * 4 + px, 4 - px
-                else:
-                    for p in rest[dy] + (1, 3):
-                        wait_a(dy * 4 + 2, p)
-                    near, p = dy * 4 + 4 - px, px
-                for q in rest[dy]:
-                    wait_a(near, q)
-                wait_a(near, p)
+                near = 4 - px if far else px
+                for p in rest + [1, 3] * far:
+                    if dy or far:
+                        wait_a(dy * 4 + 2 * far, p)
+                for q in rest:
+                    wait_a(dy * 4 + near, q)
+                wait_a(dy * 4 + near, jnp.where(near == 1, stay[0], stay[1]))
                 if at_t == 7:
                     count()
 
@@ -308,14 +307,14 @@
         for c in range(3):
             quads = (2 * c, 2 * c + 1)
             rhs = jnp.concatenate(
-                [jnp.concatenate([a_buf[slots[q // 3], p, 128 * (q % 3):128 * (q % 3 + 1), :] for q in quads], axis=1)
+                [jnp.concatenate([a_buf[slots[q // 3], p, LANES * (q % 3):LANES * (q % 3 + 1), :] for q in quads], axis=1)
                  for p in range(NP)], axis=0)
             for g in range(2):
                 prod = dot(bt[4 * n192 * g:4 * n192 * (g + 1), :], rhs)
                 for h in range(4):
                     for k2, q in enumerate(quads):
                         base = n192 * h
-                        v = [prod[base + 48 * d:base + 48 * (d + 1), 128 * k2:128 * (k2 + 1)] for d in range(4)]
+                        v = [prod[base + 48 * d:base + 48 * (d + 1), LANES * k2:LANES * (k2 + 1)] for d in range(4)]
                         for k, w in enumerate(transpose4(v)):
                             i = 4 * q + k
                             lhs2[4 * g + h, 48 * i:48 * (i + 1), :] = w.astype(BF16)
@@ -374,25 +373,19 @@
 
     lax.fori_loop(0, 8, finish, 0)
 
-    for place, p, way in sent:
-        hop(place, p, way).wait_send()
-
-    def left(t, carry):
-        for r in (1, 2, 3):
-            r_copy(t, r, 0).wait_send()
-
-        @pl.when(home != dap)
-        def _():
-            r_copy(t, 0, 0).wait_send()
-        return carry
-
-    lax.fori_loop(0, 8, left, 0)
-    for r in (1, 2, 3):
-        n_copy(r).wait_send()
+    def left(ref, sem):
+        pltpu.make_async_remote_copy(src_ref=ref, dst_ref=ref, send_sem=sem, recv_sem=n_rs.at[0, 0],
+                                     device_id=dev(col, other), device_id_type=MESH).wait_send()
+
+    left(a_buf.at[pl.ds(0, 15)], a_ss)
+    left(b_buf.at[pl.ds(0, 3)], b_ss)
+    left(r_send.at[pl.ds(0, 6)], r_ss.at[1])
+    left(n_send.at[pl.ds(0, 3)], n_ss.at[1])
 
     @pl.when(home != dap)
     def _():
-        n_copy(0).wait_send()
+        left(r_send.at[pl.ds(0, 2)], r_ss.at[0])
+        left(n_send.at[pl.ds(0, 1)], n_ss.at[0])
 
 
 def solution(mesh):
@@ -408,12 +401,12 @@
         pltpu.VMEM((HID * HID, PAIR), BF16), pltpu.VMEM((1, PAIR), BF16),
         pltpu.VMEM((NP, RES, PIECE, CH), BF16),
         pltpu.VMEM((16, SEQ), F32),
-        pltpu.VMEM((128, 4 * CH), BF16),
+        pltpu.VMEM((LANES, 4 * CH), BF16),
         pltpu.VMEM((AROWS, PIECE), F32),
-        pltpu.VMEM((16, NP, PROWS, 128), BF16),
-        pltpu.VMEM((4, NP, PROWS, 128), BF16),
+        pltpu.VMEM((16, NP, PROWS, LANES), BF16),
+        pltpu.VMEM((4, NP, PROWS, LANES), BF16),
         pltpu.VMEM((4 * AROWS, SEQ), BF16),
-        pltpu.VMEM((8, UNIT * 48, 128), BF16),
+        pltpu.VMEM((8, UNIT * 48, LANES), BF16),
         pltpu.VMEM((48 * UNIT, PAIR), F32),
         pltpu.VMEM((HID * HID, PAIR), F32),
         pltpu.VMEM((HID * HID, PAIR), BF16),
@@ -425,8 +418,7 @@
         pltpu.VMEM((2, 256, 16), F32),
         pltpu.VMEM((RES, 384, PAIR), F32),
         dma((9,)), dma((NP,)), dma,
-        dma((16, NP, 4)), dma((16, NP)), dma((4, NP, 2)), dma((4, NP)),
-        dma((8, 4)), dma((2, 2, 8)), dma((4,)), dma((2, 2)),
+        dma, dma((16, NP)), dma, dma((4, NP)), dma((2,)), dma((2, 2, 8)), dma((2,)), dma((2, 2)),
     ]
 
     def local_fn(m, mask, z, gamma, beta, w_a, b_a, w_b, b_b, w_out, b_out):

time: 59.5 us -> 56.2 us (0.945)
  Pallas kernels: 57.9 us -> 54.6 us
    pallas_call x1, Pallas kernels: 57.9 us -> 54.6 us  [local_fn(): pl.pallas_call(kernel, out_shape=pltpu.VMEM((RES, 384, PAIR), F32), in_sp...]
where the time goes in v5:
time: 56.2 us; the launch traced here: 56 us
  Pallas kernels  54.6 us (97%)
  local copies, waits for them, and re-layouts  1.41 us (3%)
    pallas_call x1, Pallas kernels, local_fn(): pl.pallas_call(kernel, out_shape=pltpu.VMEM((RES, 384, PAIR), F32), in_sp...  54.6 us
    unnamed x1, local copies, waits for them, and re-layouts  1.41 us

profile of v5, /device:TPU:1, one launch (start us, length us, event | category | flops | bytes accessed | tf_op | source)
XLA Modules:
  0.0 56.0 jit_solution(15504118543184021353)
XLA Ops:
  0.0 54.6 %opm.1 = f32[12,384,128]{2,1,0:T(8,128)S(1)} custom-call(bf16[12,512,256]{2,1,0:T(8,128)(2,1)} %bitcast.10, s32[12,512]{1,0:T(8,128)} %bitcast.12, f32[12,384,128]{2,1,0:T(8,128)} %bitcast.11, bf16[256]{0:T(256)(128)(2,1)} %gamma_hbm.1, bf16[256]{0:T(256)(128)(2,1)} %beta_hbm.1, bf16[32,256]{1,0:T(8,128)(2,1)} %bitcast.13, bf16[1,32]{1,0:T(2,128)(2,1)} %bitcast.15, ...), custom_call_target="tpu_custom_call" | custom-call | tf_op jit(solution)/shard_map/opm/pallas_call | solution.py:425
  54.6 1.4 %copy.13 = f32[384,12,128]{2,0,1:T(8,128)} copy(f32[384,12,128]{2,0,1:T(8,128)S(1)} %bitcast.9) | data formatting | bytes 4718592

commit v6 on v5

--- a/solution.py
+++ b/solution.py
@@ -363,6 +363,7 @@
                 @pl.when(jnp.logical_not((zz == 2 * dap + k) & (dap == c)))
                 def _(k=k, c=c):
                     arrive(r_recv.at[k, c, u], r_rs.at[k, c, u], r_send.at[0, 0])
+        for k in range(2):
             rows = pl.ds(pl.multiple_of(UNIT * u, 8), UNIT)
             dst = pl.ds(pl.multiple_of(192 * k + UNIT * u, 8), UNIT)
             inv = inv_v[k, rows, :]

time: 56.2 us -> 55.7 us (level)
  no operation moved by 1% of the time
where the time goes in v6:
time: 55.7 us; the launch traced here: 55.6 us
  Pallas kernels  54.2 us (97%)
  local copies, waits for them, and re-layouts  1.41 us (3%)
    pallas_call x1, Pallas kernels, local_fn(): pl.pallas_call(kernel, out_shape=pltpu.VMEM((RES, 384, PAIR), F32), in_sp...  54.2 us
    unnamed x1, local copies, waits for them, and re-layouts  1.41 us

profile of v6, /device:TPU:1, one launch (start us, length us, event | category | flops | bytes accessed | tf_op | source)
XLA Modules:
  0.0 55.6 jit_solution(7717735035279483408)
XLA Ops:
  0.0 54.2 %opm.1 = f32[12,384,128]{2,1,0:T(8,128)S(1)} custom-call(bf16[12,512,256]{2,1,0:T(8,128)(2,1)} %bitcast.10, s32[12,512]{1,0:T(8,128)} %bitcast.12, f32[12,384,128]{2,1,0:T(8,128)} %bitcast.11, bf16[256]{0:T(256)(128)(2,1)} %gamma_hbm.1, bf16[256]{0:T(256)(128)(2,1)} %beta_hbm.1, bf16[32,256]{1,0:T(8,128)(2,1)} %bitcast.13, bf16[1,32]{1,0:T(2,128)(2,1)} %bitcast.15, ...), custom_call_target="tpu_custom_call" | custom-call | tf_op jit(solution)/shard_map/opm/pallas_call | solution.py:426
  54.2 1.4 %copy.13 = f32[384,12,128]{2,0,1:T(8,128)} copy(f32[384,12,128]{2,0,1:T(8,128)S(1)} %bitcast.9) | data formatting | bytes 4718592

commit v7 on v6

--- a/solution.py
+++ b/solution.py
@@ -52,6 +52,9 @@
     return hops
 
 
+OWN = sorted({(place, p) for place, p, _ in all_hops() if any(place)})
+
+
 ORDER = {-5: (0, 1, 2, 3, 4, 5), -4: (6, 7, 8, 9, 10), -3: (17,), -2: (12, 19, 14, 15, 22, 23), -1: (18, 13, 20, 21,
     16, 11, 26, 24, 28, 30, 31, 44, 32, 33, 27, 25, 37, 51, 38, 45, 39, 40, 47, 48, 41, 42, 49, 50, 46, 34), 1: (35,
     36, 60, 61), 2: (56, 66, 53, 55, 43, 54), 3: (57, 65, 62, 29, 59, 67), 4: (64, 58, 63, 52), 5: (69, 71, 70, 68)}
@@ -72,7 +75,7 @@
            mask_ref, gamma_ref, beta_ref, wa_ref, ba_ref, wb_ref, bb_ref, wo_ref, bo_ref,
            m_v, mask_v, wabig, b32, a_buf, b_buf, bt, lhs2, rt, w32, wo_p, r_send, r_recv, n_send, n_recv,
            mask_all, inv_v, z_v,
-           in_sem, m_sem, z_sem, a_ss, a_rs, b_ss, b_rs, r_ss, r_rs, n_ss, n_rs):
+           in_sem, m_sem, z_sem, a_ss, a_rs, own_rs, b_ss, b_rs, r_ss, r_rs, n_ss, n_rs):
     col = lax.axis_index("col")
     dap = lax.axis_index("dap")
     zz, yy, xx = col // 16, (col // 4) % 4, col % 4
@@ -117,26 +120,25 @@
     bb_diag = jnp.where(eye, jnp.broadcast_to(bb_ref[...], (HID, HID)).astype(F32), 0.0).astype(BF16)
     bb_col = dot(bb_diag, jnp.ones((HID, LANES), BF16))
 
+    def landed(place, p):
+        if onward(place, p):
+            return own_rs.at[OWN.index((place, p))]
+        return b_rs.at[place[0]] if place[0] else a_rs.at[place[1] * 4 + place[2]]
+
     def hop(place, p, way):
         to = tuple((d + s) % 4 for d, s in zip(place, MOVE[way]))
         if way[0] == "z":
             return pltpu.make_async_remote_copy(
                 src_ref=b_buf.at[place[0], p], dst_ref=b_buf.at[to[0], p], send_sem=b_ss,
-                recv_sem=b_rs.at[to[0], p], device_id=dev(at(*MOVE[way]), dap), device_id_type=MESH)
+                recv_sem=landed(to, p), device_id=dev(at(*MOVE[way]), dap), device_id_type=MESH)
         src, dst = place[1] * 4 + place[2], to[1] * 4 + to[2]
         return pltpu.make_async_remote_copy(
             src_ref=a_buf.at[src, p], dst_ref=a_buf.at[dst, p], send_sem=a_ss,
-            recv_sem=a_rs.at[dst, p], device_id=dev(at(*MOVE[way]), dap), device_id_type=MESH)
-
-    def wait_a(i, p):
-        pltpu.make_async_remote_copy(
-            src_ref=a_buf.at[i, p], dst_ref=a_buf.at[i, p], send_sem=a_ss, recv_sem=a_rs.at[i, p],
-            device_id=dev(at(dx=1), dap), device_id_type=MESH).wait_recv()
-
-    def wait_b(r, p):
-        pltpu.make_async_remote_copy(
-            src_ref=b_buf.at[r, p], dst_ref=b_buf.at[r, p], send_sem=b_ss, recv_sem=b_rs.at[r, p],
-            device_id=dev(at(dz=1), dap), device_id_type=MESH).wait_recv()
+            recv_sem=landed(to, p), device_id=dev(at(*MOVE[way]), dap), device_id_type=MESH)
+
+    def wait(ref, sem):
+        pltpu.make_async_remote_copy(src_ref=ref, dst_ref=ref, send_sem=a_ss, recv_sem=sem,
+                                     device_id=dev(at(dx=1), dap), device_id_type=MESH).wait_recv()
 
     hops = all_hops()
     seen = set()
@@ -144,10 +146,8 @@
     def need(place, p):
         if any(place) and (place, p) not in seen:
             seen.add((place, p))
-            if place[0]:
-                wait_b(place[0], p)
-            else:
-                wait_a(place[1] * 4 + place[2], p)
+            buf = b_buf.at[place[0], p] if place[0] else a_buf.at[place[1] * 4 + place[2], p]
+            wait(buf, landed(place, p))
 
     def run(key):
         for i in ORDER.get(key, ()):
@@ -205,7 +205,9 @@
 
     for r in (1, 3, 2):
         for p in range(NP):
-            need((r, 0, 0), p)
+            if onward((r, 0, 0), p):
+                need((r, 0, 0), p)
+        wait(b_buf.at[r, pl.ds(0, NP if r == 2 else NP // 2)], b_rs.at[r])
     n192 = 4 * 4 * RES
     ro, co = iota((n192, n192), 0), iota((n192, n192), 1)
     want = ((ro // RES) % 4) * 48 + (ro // 48) * RES + ro % RES
@@ -237,12 +239,12 @@
     def r_copy(t, r, unit):
         return pltpu.make_async_remote_copy(
             src_ref=r_send.at[t, r], dst_ref=r_recv.at[zz % 2, dap, unit], send_sem=r_ss.at[1 if r else 0],
-            recv_sem=r_rs.at[zz % 2, dap, unit], device_id=dev(at(dz=-r), home), device_id_type=MESH)
+            recv_sem=r_rs.at[zz % 2, unit], device_id=dev(at(dz=-r), home), device_id_type=MESH)
 
     def n_copy(r):
         return pltpu.make_async_remote_copy(
             src_ref=n_send.at[r], dst_ref=n_recv.at[zz % 2, dap], send_sem=n_ss.at[1 if r else 0],
-            recv_sem=n_rs.at[zz % 2, dap], device_id=dev(at(dz=-r), home), device_id_type=MESH)
+            recv_sem=n_rs.at[zz % 2], device_id=dev(at(dz=-r), home), device_id_type=MESH)
 
     def count():
         for dy in range(4):
@@ -269,7 +271,6 @@
                     n_send[0] = part
                     n_copy(0).start()
 
-    stay = [p for d in (1, 3) for p in (1, 3) if not onward((0, 1, d), p)]
     px = 3 - 2 * (xx % 2)
 
     def place(t):
@@ -291,13 +292,11 @@
                     for p in range(NP):
                         if onward((0, dy, dx), p):
                             need((0, dy, dx), p)
-                near = 4 - px if far else px
-                for p in rest + [1, 3] * far:
-                    if dy or far:
-                        wait_a(dy * 4 + 2 * far, p)
-                for q in rest:
-                    wait_a(dy * 4 + near, q)
-                wait_a(dy * 4 + near, jnp.where(near == 1, stay[0], stay[1]))
+                near = dy * 4 + (4 - px if far else px)
+                kept = len(rest) + 2 * far
+                if kept:
+                    wait(a_buf.at[dy * 4 + 2 * far, pl.ds(0, kept)], a_rs.at[dy * 4 + 2 * far])
+                wait(a_buf.at[near, pl.ds(0, len(rest) + 1)], a_rs.at[near])
                 if at_t == 7:
                     count()
 
@@ -343,26 +342,24 @@
     pltpu.make_async_copy(z_hbm, z_v, z_sem).wait()
     bo = bo_ref[...].astype(F32)
 
-    def arrive(ref, sem, src):
-        pltpu.make_async_remote_copy(
-            src_ref=src, dst_ref=ref, send_sem=n_ss.at[0], recv_sem=sem,
-            device_id=dev(col, other), device_id_type=MESH).wait_recv()
+    def arrive(k, whole, part, sem):
+        @pl.when(zz != 2 * dap + k)
+        def _():
+            wait(whole, sem)
+
+        @pl.when(zz == 2 * dap + k)
+        def _():
+            wait(part, sem)
 
     for k in range(2):
-        for c in range(2):
-            @pl.when(jnp.logical_not((zz == 2 * dap + k) & (dap == c)))
-            def _(k=k, c=c):
-                arrive(n_recv.at[k, c], n_rs.at[k, c], n_send.at[0])
+        arrive(k, n_recv.at[k], n_recv.at[k, other], n_rs.at[k])
         inv = 1.0 / (1e-3 + (n_recv[k, 0] + n_recv[k, 1]))
         inv_v[k] = inv.T
 
     def finish(t, carry):
         _, _, u = place(t)
         for k in range(2):
-            for c in range(2):
-                @pl.when(jnp.logical_not((zz == 2 * dap + k) & (dap == c)))
-                def _(k=k, c=c):
-                    arrive(r_recv.at[k, c, u], r_rs.at[k, c, u], r_send.at[0, 0])
+            arrive(k, r_recv.at[k, pl.ds(0, 2), u], r_recv.at[k, other, u], r_rs.at[k, u])
         for k in range(2):
             rows = pl.ds(pl.multiple_of(UNIT * u, 8), UNIT)
             dst = pl.ds(pl.multiple_of(192 * k + UNIT * u, 8), UNIT)
@@ -375,7 +372,7 @@
     lax.fori_loop(0, 8, finish, 0)
 
     def left(ref, sem):
-        pltpu.make_async_remote_copy(src_ref=ref, dst_ref=ref, send_sem=sem, recv_sem=n_rs.at[0, 0],
+        pltpu.make_async_remote_copy(src_ref=ref, dst_ref=ref, send_sem=sem, recv_sem=n_rs.at[0],
                                      device_id=dev(col, other), device_id_type=MESH).wait_send()
 
     left(a_buf.at[pl.ds(0, 15)], a_ss)
@@ -419,7 +416,7 @@
         pltpu.VMEM((2, 256, 16), F32),
         pltpu.VMEM((RES, 384, PAIR), F32),
         dma((9,)), dma((NP,)), dma,
-        dma, dma((16, NP)), dma, dma((4, NP)), dma((2,)), dma((2, 2, 8)), dma((2,)), dma((2, 2)),
+        dma, dma((16,)), dma((len(OWN),)), dma, dma((4,)), dma((2,)), dma((2, 8)), dma((2,)), dma((2,)),
     ]
 
     def local_fn(m, mask, z, gamma, beta, w_a, b_a, w_b, b_b, w_out, b_out):

time: 55.7 us -> 55.2 us (level)
  no operation moved by 1% of the time
where the time goes in v7:
time: 55.2 us; the launch traced here: 55.1 us
  Pallas kernels  53.7 us (97%)
  local copies, waits for them, and re-layouts  1.41 us (3%)
    pallas_call x1, Pallas kernels, local_fn(): pl.pallas_call(kernel, out_shape=pltpu.VMEM((RES, 384, PAIR), F32), in_sp...  53.7 us
    unnamed x1, local copies, waits for them, and re-layouts  1.41 us

profile of v7, /device:TPU:1, one launch (start us, length us, event | category | flops | bytes accessed | tf_op | source)
XLA Modules:
  0.0 55.1 jit_solution(1970963484882086475)
XLA Ops:
  0.0 53.7 %opm.1 = f32[12,384,128]{2,1,0:T(8,128)S(1)} custom-call(bf16[12,512,256]{2,1,0:T(8,128)(2,1)} %bitcast.10, s32[12,512]{1,0:T(8,128)} %bitcast.12, f32[12,384,128]{2,1,0:T(8,128)} %bitcast.11, bf16[256]{0:T(256)(128)(2,1)} %gamma_hbm.1, bf16[256]{0:T(256)(128)(2,1)} %beta_hbm.1, bf16[32,256]{1,0:T(8,128)(2,1)} %bitcast.13, bf16[1,32]{1,0:T(2,128)(2,1)} %bitcast.15, ...), custom_call_target="tpu_custom_call" | custom-call | tf_op jit(solution)/shard_map/opm/pallas_call | solution.py:423
  53.7 1.4 %copy.13 = f32[384,12,128]{2,0,1:T(8,128)} copy(f32[384,12,128]{2,0,1:T(8,128)S(1)} %bitcast.9) | data formatting | bytes 4718592

commit v8 on v7

--- a/solution.py
+++ b/solution.py
@@ -74,7 +74,7 @@
            out_ref,
            mask_ref, gamma_ref, beta_ref, wa_ref, ba_ref, wb_ref, bb_ref, wo_ref, bo_ref,
            m_v, mask_v, wabig, b32, a_buf, b_buf, bt, lhs2, rt, w32, wo_p, r_send, r_recv, n_send, n_recv,
-           mask_all, inv_v, z_v,
+           mask_all, inv_v, z_v, squeeze_v,
            in_sem, m_sem, z_sem, a_ss, a_rs, own_rs, b_ss, b_rs, r_ss, r_rs, n_ss, n_rs):
     col = lax.axis_index("col")
     dap = lax.axis_index("dap")
@@ -201,6 +201,8 @@
 
     lax.fori_loop(0, HID, order, 0)
 
+    ro, co = iota((256, 256), 0), iota((256, 256), 1)
+    squeeze_v[...] = jnp.where((ro < 192) & ((ro // RES) * 16 + ro % RES == co), 1.0, 0.0).astype(BF16)
     run(-1)
 
     for r in (1, 3, 2):
@@ -246,15 +248,16 @@
             src_ref=n_send.at[r], dst_ref=n_recv.at[zz % 2, dap], send_sem=n_ss.at[1 if r else 0],
             recv_sem=n_rs.at[zz % 2], device_id=dev(at(dz=-r), home), device_id_type=MESH)
 
-    def count():
-        for dy in range(4):
+    def gather_masks(lines):
+        for dy in lines:
             for dx in range(4):
                 pos = ((yy + 4 - dy) % 4) * 4 + (xx + 4 - dx) % 4
                 mask_all[pl.ds(pl.multiple_of(16 * pos, 16), 16), :] = jnp.concatenate(
                     [a_buf[dy * 4 + dx, p, AROWS:PROWS, :] for p in range(NP)], axis=1)
-        ro, co = iota((256, 256), 0), iota((256, 256), 1)
-        squeeze = jnp.where((ro < 192) & ((ro // RES) * 16 + ro % RES == co), 1.0, 0.0).astype(BF16)
-        mask_rows = dot(squeeze, mask_all[...]).astype(BF16)
+
+    def count():
+        gather_masks((STEPS[7][0],))
+        mask_rows = dot(squeeze_v[...], mask_all[...]).astype(BF16)
         for r in range(4):
             mask_cols = jnp.concatenate([b_buf[r, p, AROWS:PROWS, :] for p in range(NP)], axis=1)
             part = dot(mask_cols, mask_rows, NT)
@@ -297,6 +300,8 @@
                 if kept:
                     wait(a_buf.at[dy * 4 + 2 * far, pl.ds(0, kept)], a_rs.at[dy * 4 + 2 * far])
                 wait(a_buf.at[near, pl.ds(0, len(rest) + 1)], a_rs.at[near])
+                if at_t == 6:
+                    gather_masks([d for d in range(4) if d != dy])
                 if at_t == 7:
                     count()
 
@@ -414,7 +419,7 @@
         pltpu.VMEM((2, 2, 16, 256), F32),
         pltpu.VMEM((256, SEQ), BF16),
         pltpu.VMEM((2, 256, 16), F32),
-        pltpu.VMEM((RES, 384, PAIR), F32),
+        pltpu.VMEM((RES, 384, PAIR), F32), pltpu.VMEM((256, 256), BF16),
         dma((9,)), dma((NP,)), dma,
         dma, dma((16,)), dma((len(OWN),)), dma, dma((4,)), dma((2,)), dma((2, 8)), dma((2,)), dma((2,)),
     ]

time: 55.2 us -> 55.2 us (level)
  no operation moved by 1% of the time
where the time goes in v8:
time: 55.2 us; the launch traced here: 55.1 us
  Pallas kernels  53.7 us (97%)
  local copies, waits for them, and re-layouts  1.41 us (3%)
    pallas_call x1, Pallas kernels, local_fn(): pl.pallas_call(kernel, out_shape=pltpu.VMEM((RES, 384, PAIR), F32), in_sp...  53.7 us
    unnamed x1, local copies, waits for them, and re-layouts  1.41 us

profile of v8, /device:TPU:1, one launch (start us, length us, event | category | flops | bytes accessed | tf_op | source)
XLA Modules:
  0.0 55.1 jit_solution(13889064986253144117)
XLA Ops:
  0.0 53.7 %opm.1 = f32[12,384,128]{2,1,0:T(8,128)S(1)} custom-call(bf16[12,512,256]{2,1,0:T(8,128)(2,1)} %bitcast.10, s32[12,512]{1,0:T(8,128)} %bitcast.12, f32[12,384,128]{2,1,0:T(8,128)} %bitcast.11, bf16[256]{0:T(256)(128)(2,1)} %gamma_hbm.1, bf16[256]{0:T(256)(128)(2,1)} %beta_hbm.1, bf16[32,256]{1,0:T(8,128)(2,1)} %bitcast.13, bf16[1,32]{1,0:T(2,128)(2,1)} %bitcast.15, ...), custom_call_target="tpu_custom_call" | custom-call | tf_op jit(solution)/shard_map/opm/pallas_call | solution.py:428
  53.7 1.4 %copy.13 = f32[384,12,128]{2,0,1:T(8,128)} copy(f32[384,12,128]{2,0,1:T(8,128)S(1)} %bitcast.9) | data formatting | bytes 4718592
